TPU v7x, 256 devices: a 2x2x32 block of a 4x8x32 slice. The times are simulated.
256 devices in a mesh: tiles: 4 (over x, y), rows: 32 (over z), dates: 2 (over core).
Axes of the slice: x: 2, y: 2, z: 32, core: 2. Of those that a mesh axis runs over, the one named last changes fastest.
The devices are a block of a 4x8x32 slice.
Arguments:
- red_band: int32 [24, 4096, 2048], P('dates', ('tiles', 'rows')), parts along dimension 1, may hold values from 1 to 1073741823
- nir_band: int32 [24, 4096, 2048], P('dates', ('tiles', 'rows')), parts along dimension 1, may hold values from 1 to 1073741823
- cloud_class: int32 [24, 4096, 2048], P('dates', ('tiles', 'rows')), parts along dimension 1, may hold values from 0 to 3
- date_ordinal: int32 [96], P(('tiles', 'dates')), parts along dimension 0, may hold values from 0 to 23, each once
Outputs:
- composite_red: int32 [4096, 2048], P(('tiles', 'rows', 'dates')), parts along dimension 0
- composite_nir: int32 [4096, 2048], P(('tiles', 'rows', 'dates')), parts along dimension 0
- chosen_date: int32 [4096, 2048], P(('tiles', 'rows', 'dates')), parts along dimension 0
- overview_one: float32 [2, 2048, 1024], P(None, ('tiles', 'rows', 'dates')), parts along dimension 1
- overview_two: float32 [2, 1024, 512], P(None, ('tiles', 'rows', 'dates')), parts along dimension 1
- overview_three: float32 [2, 512, 256], P(None, ('tiles', 'rows', 'dates')), parts along dimension 1
There are 4 independent parts, one for each index of `tiles`. A program takes and returns all parts, laid end to end along the dimension named above; each array names one. Nothing has to cross between parts.
Inputs may be any that keep to these rules, and one draw needn't show every extreme that they name: `date_ordinal`: each ordinal appears once.
All inputs are finite; a program needn't handle non-finite values.
Results may differ from a plain program's by a relative error of at most 0.0003.
Values sent between devices are 32-bit elements; how exact they have to be, the bound alone decides.
A program may use at most 192 MiB of HBM per device.

v0:
```python
import jax
import jax.numpy as jnp
from jax import lax
from jax.sharding import PartitionSpec as P

LEVELS = 3


KERNEL = (0.0625, 0.25, 0.375, 0.25, 0.0625)
LIMB = 32768
TWO_LIMBS = 1073741824
SCALE_BAND = 9.313225746154785e-10
FLAG_STEP = 32


def merged_2(value, axis, join):
    pieces = jax.tree.map(lambda part: lax.all_gather(part, axis), value)
    head = jax.tree.map(lambda part: part[0], pieces)
    tail = jax.tree.map(lambda part: part[1:], pieces)
    so_far, _ = lax.scan(lambda so_far, section: (join(so_far, section), None), head, tail)
    return so_far


def extended(value, sides, width):
    edges = {}
    for axis, dim in sides:
        peers, length = (lax.axis_size(axis), value.shape[dim])
        up = [(i, (i + 1) % peers) for i in range(peers - 1)]
        last = lax.slice_in_dim(value, length - width, length, axis=dim)
        first = lax.slice_in_dim(value, 0, width, axis=dim)
        edges[dim] = (
            lax.ppermute(last, axis, up),
            lax.ppermute(first, axis, [(b, a) for a, b in up]),
        )
    done = []
    for _, dim in sides:
        low, high = edges[dim]
        around = [(width, width) if d in done else (0, 0) for d in range(value.ndim)]
        value = jnp.concatenate([jnp.pad(low, around), value, jnp.pad(high, around)], axis=dim)
        done.append(dim)
    return value


def product_digits(small, large):
    small_hi = small // LIMB
    small_lo = small % LIMB
    large_top = large // TWO_LIMBS
    remain = large % TWO_LIMBS
    large_mid = remain // LIMB
    large_lo = remain % LIMB
    digit_zero = small_lo * large_lo
    digit_one = small_hi * large_lo + small_lo * large_mid
    digit_two = small_hi * large_mid + small_lo * large_top
    digit_three = small_hi * large_top
    digit_one = digit_one + digit_zero // LIMB
    digit_zero = digit_zero % LIMB
    digit_two = digit_two + digit_one // LIMB
    digit_one = digit_one % LIMB
    digit_three = digit_three + digit_two // LIMB
    digit_two = digit_two % LIMB
    return (digit_three, digit_two, digit_one, digit_zero)


def compare_digits(first, second):
    greater = first[0] > second[0]
    equal = first[0] == second[0]
    for one, two in zip(first[1:], second[1:]):
        greater = greater | equal & (one > two)
        equal = equal & (one == two)
    return (greater, equal)


def better(first, second):
    clear_a, red_a, nir_a, ord_a = first
    clear_b, red_b, nir_b, ord_b = second
    diff_a = nir_a - red_a
    diff_b = nir_b - red_b
    total_a = nir_a + red_a
    total_b = nir_b + red_b
    sign_a = jnp.sign(diff_a)
    sign_b = jnp.sign(diff_b)
    greater, equal = compare_digits(
        product_digits(jnp.abs(diff_a), total_b), product_digits(jnp.abs(diff_b), total_a)
    )
    lesser = jnp.logical_not(greater | equal)
    same_sign = sign_a == sign_b
    ndvi_more = (sign_a > sign_b) | same_sign & ((sign_a > 0) & greater | (sign_a < 0) & lesser)
    ndvi_same = same_sign & ((sign_a == 0) | equal)
    same_clear = clear_a == clear_b
    take = (clear_a > clear_b) | same_clear & (ndvi_more | ndvi_same & (ord_a < ord_b))
    return tuple((jnp.where(take, one, two) for one, two in zip(first, second)))


def fold_flag(entries):
    clear, red, nir, ordinal = entries
    return (red, nir, ordinal + FLAG_STEP * clear)


def unfold_flag(packed):
    red, nir, flagged = packed
    clear = (flagged >= FLAG_STEP).astype(jnp.int32)
    return (clear, red, nir, flagged - FLAG_STEP * clear)


def better_packed(first, second):
    return fold_flag(better(unfold_flag(first), unfold_flag(second)))


def smooth_pool(padded, rows):
    cols = padded.shape[2]
    smooth = KERNEL[0] * padded[:, 0:rows]
    for offset in range(1, 5):
        smooth = smooth + KERNEL[offset] * padded[:, offset : offset + rows]
    widened = jnp.pad(smooth, ((0, 0), (0, 0), (2, 2)))
    result = KERNEL[0] * widened[:, :, 0:cols]
    for offset in range(1, 5):
        result = result + KERNEL[offset] * widened[:, :, offset : offset + cols]
    return result.reshape(2, rows // 2, 2, cols // 2, 2).mean(axis=(2, 4))


def body(red_band, nir_band, cloud_class, date_ordinal):
    strip = red_band.shape[1]
    half = strip // 2

    def entry(index):
        return (
            (cloud_class[index] == 0).astype(jnp.int32),
            red_band[index],
            nir_band[index],
            jnp.full(red_band.shape[1:], date_ordinal[index], jnp.int32),
        )

    def advance(carry, index):
        return (better(carry, entry(index)), None)

    best, unused = lax.scan(advance, entry(0), jnp.arange(1, red_band.shape[0], dtype=jnp.int32))
    outgoing = fold_flag(best)
    merged = merged_2(outgoing, "dates", better_packed)
    begin = lax.axis_index("dates") * half
    chosen = tuple((lax.dynamic_slice_in_dim(member, begin, half, 0) for member in merged))
    mine = unfold_flag(chosen)
    level = jnp.stack([mine[1], mine[2]]).astype(jnp.float32) * SCALE_BAND
    levels = []
    for number in range(LEVELS):
        rows = level.shape[1]
        padded = extended(level, ((("rows", "dates"), 1),), 2)
        level = smooth_pool(padded, rows)
        levels.append(level)
    return (mine[1], mine[2], mine[3], levels[0], levels[1], levels[2])


def solution(mesh):
    in_specs = (
        P("dates", ("tiles", "rows"), None),
        P("dates", ("tiles", "rows"), None),
        P("dates", ("tiles", "rows"), None),
        P(("tiles", "dates")),
    )
    out_specs = (
        P(("tiles", "rows", "dates"), None),
        P(("tiles", "rows", "dates"), None),
        P(("tiles", "rows", "dates"), None),
        P(None, ("tiles", "rows", "dates"), None),
        P(None, ("tiles", "rows", "dates"), None),
        P(None, ("tiles", "rows", "dates"), None),
    )
    return jax.shard_map(body, mesh=mesh, in_specs=in_specs, out_specs=out_specs, check_vma=False)
```

profile of v0, /device:TPU:37, one launch (start us, length us, event | category | flops | bytes accessed | tf_op | source)
XLA Modules:
  0.0 208.8 jit_solution(12381239483887552990)
XLA Ops:
  3.4 113.1 %while.6 = (s32[]{:T(128)}, s32[32,2048]{1,0:T(8,128)S(1)}, s32[32,2048]{1,0:T(8,128)S(1)}, s32[32,2048]{1,0:T(8,128)S(1)}, s32[32,2048]{1,0:T(8,128)S(1)}, /*in...) while((s32[]{:T(128)}, s32[32,2048]{1,0:T(8,128)S(1)}, ...), condition=%wide.region_1.2_spmd, body=%wide.region_0.1_spmd.sunk | while | flops 19857412 | bytes 4456651 | solution.py:136
  7.2 5.3 %broadcast_select_fusion.2 = (s32[32,2048]{1,0:T(8,128)S(1)}, pred[32,2048]{1,0:T(8,128)(4,1)S(1)}, pred[1,32,2048]{2,1,0:T(8,128)(4,1)S(1)}) fusion(s32[32,2048]{1,0:T(8,128)S(1)} %get-tuple-element.353, s32[]{:T(128)} %bitcast.46, s32[32,2048]{1,0:T(8,128)S(1)} %get-tuple-element.352, s32[32,2048]{1,0:T(8,128)S(1)} %get-tuple-element.351, ...), kind=kLoop, calls=%fused_computation.107.clone.1 | loop fusion | flops 19595264 | bytes 2228232 | tf_op jit(solution)/shard_map/while/body/eval_jaxpr/jit(_where)/select_n | solution.py:91
  17.4 5.3 %broadcast_select_fusion.2 = (s32[32,2048]{1,0:T(8,128)S(1)}, pred[32,2048]{1,0:T(8,128)(4,1)S(1)}, pred[1,32,2048]{2,1,0:T(8,128)(4,1)S(1)}) fusion(s32[32,2048]{1,0:T(8,128)S(1)} %get-tuple-element.353, s32[]{:T(128)} %bitcast.46, s32[32,2048]{1,0:T(8,128)S(1)} %get-tuple-element.352, s32[32,2048]{1,0:T(8,128)S(1)} %get-tuple-element.351, ...), kind=kLoop, calls=%fused_computation.107.clone.1 | loop fusion | flops 19595264 | bytes 2228232 | tf_op jit(solution)/shard_map/while/body/eval_jaxpr/jit(_where)/select_n | solution.py:91
  27.7 5.3 %broadcast_select_fusion.2 = (s32[32,2048]{1,0:T(8,128)S(1)}, pred[32,2048]{1,0:T(8,128)(4,1)S(1)}, pred[1,32,2048]{2,1,0:T(8,128)(4,1)S(1)}) fusion(s32[32,2048]{1,0:T(8,128)S(1)} %get-tuple-element.353, s32[]{:T(128)} %bitcast.46, s32[32,2048]{1,0:T(8,128)S(1)} %get-tuple-element.352, s32[32,2048]{1,0:T(8,128)S(1)} %get-tuple-element.351, ...), kind=kLoop, calls=%fused_computation.107.clone.1 | loop fusion | flops 19595264 | bytes 2228232 | tf_op jit(solution)/shard_map/while/body/eval_jaxpr/jit(_where)/select_n | solution.py:91
  38.0 5.3 %broadcast_select_fusion.2 = (s32[32,2048]{1,0:T(8,128)S(1)}, pred[32,2048]{1,0:T(8,128)(4,1)S(1)}, pred[1,32,2048]{2,1,0:T(8,128)(4,1)S(1)}) fusion(s32[32,2048]{1,0:T(8,128)S(1)} %get-tuple-element.353, s32[]{:T(128)} %bitcast.46, s32[32,2048]{1,0:T(8,128)S(1)} %get-tuple-element.352, s32[32,2048]{1,0:T(8,128)S(1)} %get-tuple-element.351, ...), kind=kLoop, calls=%fused_computation.107.clone.1 | loop fusion | flops 19595264 | bytes 2228232 | tf_op jit(solution)/shard_map/while/body/eval_jaxpr/jit(_where)/select_n | solution.py:91
  48.3 5.3 %broadcast_select_fusion.2 = (s32[32,2048]{1,0:T(8,128)S(1)}, pred[32,2048]{1,0:T(8,128)(4,1)S(1)}, pred[1,32,2048]{2,1,0:T(8,128)(4,1)S(1)}) fusion(s32[32,2048]{1,0:T(8,128)S(1)} %get-tuple-element.353, s32[]{:T(128)} %bitcast.46, s32[32,2048]{1,0:T(8,128)S(1)} %get-tuple-element.352, s32[32,2048]{1,0:T(8,128)S(1)} %get-tuple-element.351, ...), kind=kLoop, calls=%fused_computation.107.clone.1 | loop fusion | flops 19595264 | bytes 2228232 | tf_op jit(solution)/shard_map/while/body/eval_jaxpr/jit(_where)/select_n | solution.py:91
  58.6 5.3 %broadcast_select_fusion.2 = (s32[32,2048]{1,0:T(8,128)S(1)}, pred[32,2048]{1,0:T(8,128)(4,1)S(1)}, pred[1,32,2048]{2,1,0:T(8,128)(4,1)S(1)}) fusion(s32[32,2048]{1,0:T(8,128)S(1)} %get-tuple-element.353, s32[]{:T(128)} %bitcast.46, s32[32,2048]{1,0:T(8,128)S(1)} %get-tuple-element.352, s32[32,2048]{1,0:T(8,128)S(1)} %get-tuple-element.351, ...), kind=kLoop, calls=%fused_computation.107.clone.1 | loop fusion | flops 19595264 | bytes 2228232 | tf_op jit(solution)/shard_map/while/body/eval_jaxpr/jit(_where)/select_n | solution.py:91
  68.9 5.3 %broadcast_select_fusion.2 = (s32[32,2048]{1,0:T(8,128)S(1)}, pred[32,2048]{1,0:T(8,128)(4,1)S(1)}, pred[1,32,2048]{2,1,0:T(8,128)(4,1)S(1)}) fusion(s32[32,2048]{1,0:T(8,128)S(1)} %get-tuple-element.353, s32[]{:T(128)} %bitcast.46, s32[32,2048]{1,0:T(8,128)S(1)} %get-tuple-element.352, s32[32,2048]{1,0:T(8,128)S(1)} %get-tuple-element.351, ...), kind=kLoop, calls=%fused_computation.107.clone.1 | loop fusion | flops 19595264 | bytes 2228232 | tf_op jit(solution)/shard_map/while/body/eval_jaxpr/jit(_where)/select_n | solution.py:91
  79.2 5.3 %broadcast_select_fusion.2 = (s32[32,2048]{1,0:T(8,128)S(1)}, pred[32,2048]{1,0:T(8,128)(4,1)S(1)}, pred[1,32,2048]{2,1,0:T(8,128)(4,1)S(1)}) fusion(s32[32,2048]{1,0:T(8,128)S(1)} %get-tuple-element.353, s32[]{:T(128)} %bitcast.46, s32[32,2048]{1,0:T(8,128)S(1)} %get-tuple-element.352, s32[32,2048]{1,0:T(8,128)S(1)} %get-tuple-element.351, ...), kind=kLoop, calls=%fused_computation.107.clone.1 | loop fusion | flops 19595264 | bytes 2228232 | tf_op jit(solution)/shard_map/while/body/eval_jaxpr/jit(_where)/select_n | solution.py:91
  89.5 5.3 %broadcast_select_fusion.2 = (s32[32,2048]{1,0:T(8,128)S(1)}, pred[32,2048]{1,0:T(8,128)(4,1)S(1)}, pred[1,32,2048]{2,1,0:T(8,128)(4,1)S(1)}) fusion(s32[32,2048]{1,0:T(8,128)S(1)} %get-tuple-element.353, s32[]{:T(128)} %bitcast.46, s32[32,2048]{1,0:T(8,128)S(1)} %get-tuple-element.352, s32[32,2048]{1,0:T(8,128)S(1)} %get-tuple-element.351, ...), kind=kLoop, calls=%fused_computation.107.clone.1 | loop fusion | flops 19595264 | bytes 2228232 | tf_op jit(solution)/shard_map/while/body/eval_jaxpr/jit(_where)/select_n | solution.py:91
  99.7 5.3 %broadcast_select_fusion.2 = (s32[32,2048]{1,0:T(8,128)S(1)}, pred[32,2048]{1,0:T(8,128)(4,1)S(1)}, pred[1,32,2048]{2,1,0:T(8,128)(4,1)S(1)}) fusion(s32[32,2048]{1,0:T(8,128)S(1)} %get-tuple-element.353, s32[]{:T(128)} %bitcast.46, s32[32,2048]{1,0:T(8,128)S(1)} %get-tuple-element.352, s32[32,2048]{1,0:T(8,128)S(1)} %get-tuple-element.351, ...), kind=kLoop, calls=%fused_computation.107.clone.1 | loop fusion | flops 19595264 | bytes 2228232 | tf_op jit(solution)/shard_map/while/body/eval_jaxpr/jit(_where)/select_n | solution.py:91
  110.0 5.3 %broadcast_select_fusion.2 = (s32[32,2048]{1,0:T(8,128)S(1)}, pred[32,2048]{1,0:T(8,128)(4,1)S(1)}, pred[1,32,2048]{2,1,0:T(8,128)(4,1)S(1)}) fusion(s32[32,2048]{1,0:T(8,128)S(1)} %get-tuple-element.353, s32[]{:T(128)} %bitcast.46, s32[32,2048]{1,0:T(8,128)S(1)} %get-tuple-element.352, s32[32,2048]{1,0:T(8,128)S(1)} %get-tuple-element.351, ...), kind=kLoop, calls=%fused_computation.107.clone.1 | loop fusion | flops 19595264 | bytes 2228232 | tf_op jit(solution)/shard_map/while/body/eval_jaxpr/jit(_where)/select_n | solution.py:91
  116.6 22.3 %all-gather = s32[64,2048]{1,0:T(8,128)S(1)} all-gather(s32[32,2048]{1,0:T(8,128)S(1)} %multiply_add_fusion.1), channel_id=2, replica_groups=mesh['tiles'=4,'rows'=32,'dates'=2] {'dates'}, dimensions={0}, use_global_device_ids=true | all-gather | bytes 786432 | tf_op jit(solution)/shard_map/all_gather | solution.py:17
  144.1 3.5 %fusion.105 = (s32[32,2048]{1,0:T(8,128)S(1)}, pred[32,2048]{1,0:T(8,128)(4,1)S(1)}, s32[32,2048]{1,0:T(8,128)S(1)}) fusion(pred[32,2048]{1,0:T(8,128)(4,1)S(1)} %get-tuple-element.237, pred[32,2048]{1,0:T(8,128)(4,1)S(1)} %get-tuple-element.246, s32[64,2048]{1,0:T(8,128)S(1)} %all-gather, s32[64,2048]{1,0:T(8,128)S(1)} %all-gather.2, ...), kind=kLoop, calls=%fused_computation.307 | loop fusion | flops 19791872 | bytes 2293760 | tf_op jit(solution)/shard_map/while/body/eval_jaxpr/convert_element_type | solution.py:101
  151.3 2.6 %collective-permute-start.1 = (f32[2,2,2048]{2,1,0:T(2,128)S(1)}, f32[2,2,2048]{2,1,0:T(2,128)S(1)}, u32[]{:S(2)}, u32[]{:S(2)}) collective-permute-start(f32[2,2,2048]{2,1,0:T(2,128)S(1)} %get-tuple-element.250), channel_id=1, source_target_pairs={{1,0},{2,1},{3,2},{4,3},{5,4},{6,5},{7,6},{8,7},{9,8},{10,9},{11,1... | collective-permute-start | bytes 98312 | tf_op jit(solution)/shard_map/ppermute | solution.py:33
  153.9 2.6 %collective-permute-done.1 = f32[2,2,2048]{2,1,0:T(2,128)S(1)} collective-permute-done((f32[2,2,2048]{2,1,0:T(2,128)S(1)}, f32[2,2,2048]{2,1,0:T(2,128)S(1)}, u32[]{:S(2)}, u32[]{:S(2)}) %collective-permute-start.1) | collective-permute-done | bytes 32800 | tf_op jit(solution)/shard_map/ppermute | solution.py:33
  157.1 19.0 %reshape.29 = f32[2,8,2,1024,2]{4,3,2,1,0:T(8,128)} reshape(f32[2,16,2048]{2,1,0:T(8,128)S(1)} %multiply_add_fusion) | data formatting | bytes 524288 | tf_op jit(solution)/shard_map/reshape | solution.py:118
  176.1 8.0 %reduce_sum.27 = f32[2,8,1024]{2,1,0:T(8,128)S(1)} reduce(f32[2,8,2,1024,2]{4,3,2,1,0:T(8,128)} %reshape.29, f32[]{:T(128)} %constant.498.clone.1), dimensions={2,4}, to_apply=%region_2.3 | reduce | flops 49152 | bytes 327684 | tf_op jit(solution)/shard_map/reduce_sum | solution.py:118
  186.1 2.4 %collective-permute-start.3 = (f32[2,2,1024]{2,1,0:T(2,128)S(1)}, f32[2,2,1024]{2,1,0:T(2,128)S(1)}, u32[]{:S(2)}, u32[]{:S(2)}) collective-permute-start(f32[2,2,1024]{2,1,0:T(2,128)S(1)} %get-tuple-element.252), channel_id=1, source_target_pairs={{1,0},{2,1},{3,2},{4,3},{5,4},{6,5},{7,6},{8,7},{9,8},{10,9},{11,1... | collective-permute-start | bytes 49160 | tf_op jit(solution)/shard_map/ppermute | solution.py:33
  188.6 2.6 %collective-permute-done.3 = f32[2,2,1024]{2,1,0:T(2,128)S(1)} collective-permute-done((f32[2,2,1024]{2,1,0:T(2,128)S(1)}, f32[2,2,1024]{2,1,0:T(2,128)S(1)}, u32[]{:S(2)}, u32[]{:S(2)}) %collective-permute-start.3) | collective-permute-done | bytes 16416 | tf_op jit(solution)/shard_map/ppermute | solution.py:33
  191.4 5.5 %reshape.30 = f32[2,4,2,512,2]{4,3,2,1,0:T(8,128)} reshape(f32[2,8,1024]{2,1,0:T(8,128)S(1)} %fusion.68) | data formatting | bytes 131072 | tf_op jit(solution)/shard_map/reshape | solution.py:118
  196.9 2.8 %reduce_sum.28 = f32[2,4,512]{2,1,0:T(4,128)S(1)} reduce(f32[2,4,2,512,2]{4,3,2,1,0:T(8,128)} %reshape.30, f32[]{:T(128)} %constant.498.clone.1), dimensions={2,4}, to_apply=%region_3.4 | reduce | flops 12288 | bytes 81924 | tf_op jit(solution)/shard_map/reduce_sum | solution.py:118
  201.8 2.4 %collective-permute-start.5 = (f32[2,2,512]{2,1,0:T(2,128)S(1)}, f32[2,2,512]{2,1,0:T(2,128)S(1)}, u32[]{:S(2)}, u32[]{:S(2)}) collective-permute-start(f32[2,2,512]{2,1,0:T(2,128)S(1)} %get-tuple-element.260), channel_id=1, source_target_pairs={{1,0},{2,1},{3,2},{4,3},{5,4},{6,5},{7,6},{8,7},{9,8},{10,9},{11,1... | collective-permute-start | bytes 24584 | tf_op jit(solution)/shard_map/ppermute | solution.py:33
  204.2 2.6 %collective-permute-done.5 = f32[2,2,512]{2,1,0:T(2,128)S(1)} collective-permute-done((f32[2,2,512]{2,1,0:T(2,128)S(1)}, f32[2,2,512]{2,1,0:T(2,128)S(1)}, u32[]{:S(2)}, u32[]{:S(2)}) %collective-permute-start.5) | collective-permute-done | bytes 8224 | tf_op jit(solution)/shard_map/ppermute | solution.py:33
  (73 shorter events, 52.0 us)
Async XLA Ops:
  149.3 26.8 %copy-start = (s32[16,2048]{1,0:T(8,128)}, s32[16,2048]{1,0:T(8,128)S(1)}, u32[]{:S(2)}) copy-start(s32[16,2048]{1,0:T(8,128)S(1)} %get-tuple-element.254) | copy-start | bytes 393220
  149.3 26.8 %copy-start.1 = (s32[16,2048]{1,0:T(8,128)}, s32[16,2048]{1,0:T(8,128)S(1)}, u32[]{:S(2)}) copy-start(s32[16,2048]{1,0:T(8,128)S(1)} %get-tuple-element.255) | copy-start | bytes 393220
  149.3 4.6 %collective-permute-start = (f32[2,2,2048]{2,1,0:T(2,128)S(1)}, f32[2,2,2048]{2,1,0:T(2,128)S(1)}, u32[]{:S(2)}, u32[]{:S(2)}) collective-permute-start(f32[2,2,2048]{2,1,0:T(2,128)S(1)} %get-tuple-element.249), channel_id=1, source_target_pairs={{0,1},{1,2},{2,3},{3,4},{4,5},{5,6},{6,7},{7,8},{8,9},{9,10},{10,1... | collective-permute-start | bytes 98312 | tf_op jit(solution)/shard_map/ppermute | solution.py:32
  151.3 5.3 %collective-permute-start.1 = (f32[2,2,2048]{2,1,0:T(2,128)S(1)}, f32[2,2,2048]{2,1,0:T(2,128)S(1)}, u32[]{:S(2)}, u32[]{:S(2)}) collective-permute-start(f32[2,2,2048]{2,1,0:T(2,128)S(1)} %get-tuple-element.250), channel_id=1, source_target_pairs={{1,0},{2,1},{3,2},{4,3},{5,4},{6,5},{7,6},{8,7},{9,8},{10,9},{11,1... | collective-permute-start | bytes 98312 | tf_op jit(solution)/shard_map/ppermute | solution.py:33
  184.1 15.6 %copy-start.2 = (f32[2,8,1024]{2,1,0:T(8,128)}, f32[2,8,1024]{2,1,0:T(8,128)S(1)}, u32[]{:S(2)}) copy-start(f32[2,8,1024]{2,1,0:T(8,128)S(1)} %broadcast_multiply_fusion) | copy-start | bytes 196612
  184.2 4.4 %collective-permute-start.2 = (f32[2,2,1024]{2,1,0:T(2,128)S(1)}, f32[2,2,1024]{2,1,0:T(2,128)S(1)}, u32[]{:S(2)}, u32[]{:S(2)}) collective-permute-start(f32[2,2,1024]{2,1,0:T(2,128)S(1)} %get-tuple-element.251), channel_id=1, source_target_pairs={{0,1},{1,2},{2,3},{3,4},{4,5},{5,6},{6,7},{7,8},{8,9},{9,10},{10,1... | collective-permute-start | bytes 49160 | tf_op jit(solution)/shard_map/ppermute | solution.py:32
  186.1 5.1 %collective-permute-start.3 = (f32[2,2,1024]{2,1,0:T(2,128)S(1)}, f32[2,2,1024]{2,1,0:T(2,128)S(1)}, u32[]{:S(2)}, u32[]{:S(2)}) collective-permute-start(f32[2,2,1024]{2,1,0:T(2,128)S(1)} %get-tuple-element.252), channel_id=1, source_target_pairs={{1,0},{2,1},{3,2},{4,3},{5,4},{6,5},{7,6},{8,7},{9,8},{10,9},{11,1... | collective-permute-start | bytes 49160 | tf_op jit(solution)/shard_map/ppermute | solution.py:33
  199.8 9.0 %copy-start.3 = (f32[2,4,512]{2,1,0:T(4,128)}, f32[2,4,512]{2,1,0:T(4,128)S(1)}, u32[]{:S(2)}) copy-start(f32[2,4,512]{2,1,0:T(4,128)S(1)} %broadcast_multiply_fusion.1) | copy-start | bytes 49156
  199.8 4.4 %collective-permute-start.4 = (f32[2,2,512]{2,1,0:T(2,128)S(1)}, f32[2,2,512]{2,1,0:T(2,128)S(1)}, u32[]{:S(2)}, u32[]{:S(2)}) collective-permute-start(f32[2,2,512]{2,1,0:T(2,128)S(1)} %get-tuple-element.259), channel_id=1, source_target_pairs={{0,1},{1,2},{2,3},{3,4},{4,5},{5,6},{6,7},{7,8},{8,9},{9,10},{10,1... | collective-permute-start | bytes 24584 | tf_op jit(solution)/shard_map/ppermute | solution.py:32
  201.8 5.0 %collective-permute-start.5 = (f32[2,2,512]{2,1,0:T(2,128)S(1)}, f32[2,2,512]{2,1,0:T(2,128)S(1)}, u32[]{:S(2)}, u32[]{:S(2)}) collective-permute-start(f32[2,2,512]{2,1,0:T(2,128)S(1)} %get-tuple-element.260), channel_id=1, source_target_pairs={{1,0},{2,1},{3,2},{4,3},{5,4},{6,5},{7,6},{8,7},{9,8},{10,9},{11,1... | collective-permute-start | bytes 24584 | tf_op jit(solution)/shard_map/ppermute | solution.py:33
where the time goes:
time: 210 us; the launch traced here: 209 us
  other arithmetic  91 us (43%)
  local copies, waits for them, and re-layouts  47.5 us (23%)
  blocking collectives  26.7 us (13%)
  loops' own time  21.6 us (10%)
  starting transfers between devices  13.3 us (6%)
  waiting for transfers between devices  7.84 us (4%)
    select_n x22, other arithmetic, better(): return tuple((jnp.where(take, one, two) for one, two in zip(first, second)))  71.4 us
    all_gather x3, blocking collectives, merged_2(): pieces = jax.tree.map(lambda part: lax.all_gather(part, axis), value)  26.7 us
    reshape x3, local copies, waits for them, and re-layouts, smooth_pool(): return result.reshape(2, rows // 2, 2, cols // 2, 2).mean(axis=(2, 4))  25.5 us
    another operation x1, loops' own time, body(): lax.scan(advance, entry(0), jnp.arange(1, red_band.shape[0], dtype=jnp.in...  21.6 us
    dynamic_slice x11, local copies, waits for them, and re-layouts, entry(): date_ordinal[index]  13.7 us
    reduce_sum x3, other arithmetic, smooth_pool(): return result.reshape(2, rows // 2, 2, cols // 2, 2).mean(axis=(2, 4))  11 us
    ppermute x3, waiting for transfers between devices, extended(): lax.ppermute(first, axis, [(b, a) for a, b in up])  7.83 us
    ppermute x3, starting transfers between devices, extended(): lax.ppermute(first, axis, [(b, a) for a, b in up])  7.47 us
  transfers between devices with their start and end apart: 6, of which 3 were waited for; matrix products, arithmetic and copies ran while one was open for 0% of the time, Pallas kernels for 0%

commit v1 on v0

v1 whole, which is shorter than its diff:
```python
import functools

import jax
import jax.numpy as jnp
from jax import lax
from jax.experimental import pallas as pl
from jax.experimental.pallas import tpu as pltpu
from jax.sharding import PartitionSpec as P

MESH = pl.DeviceIdType.MESH
LIMB_BITS = 15
LIMB_MASK = 32767
CLEAR = 1 << 30
FLAG_STEP = 32
SCALE_BAND = 9.313225746154785e-10
TAPS = (0.03125, 0.15625, 0.3125, 0.3125, 0.15625, 0.03125)
TILE = 8
GROUP = 512
SPAN = 256
WINDOW = 2 * SPAN + 256


def split(value):
    return value >> LIMB_BITS, value & LIMB_MASK


def join(high, low):
    return (high << LIMB_BITS) | low


def improve(best, new):
    n1, n0, r1, r0, clear, order = best
    m1, m0, s1, s0, fresh, index = new
    low = m0 * r0 - n0 * s0 + ((order - index) >> 31)
    mid = (m1 * r0 + m0 * r1) - (n1 * s0 + n0 * s1) + (low >> LIMB_BITS)
    top = m1 * r1 - n1 * s1 + (mid >> LIMB_BITS) + (fresh - clear)
    take = top >= 0
    return tuple(jnp.where(take, one, two) for one, two in zip(new, best))


def pooled(window, weights):
    parts = []
    for block in window:
        head = block.astype(jnp.bfloat16)
        parts += [head, (block - head.astype(jnp.float32)).astype(jnp.bfloat16)]
    rows = window[0].shape[0]
    out = jnp.dot(jnp.concatenate(parts, axis=0), weights, preferred_element_type=jnp.float32)
    return [out[2 * b * rows : (2 * b + 1) * rows] + out[(2 * b + 1) * rows : (2 * b + 2) * rows] for b in range(len(window))]


def kernel(
    ordinal, red, nir, cloud,
    comp_red, comp_nir, chosen, one, two, three,
    in_red, in_nir, in_cloud, sent, got, level, ext, weights, level1, ext1, level2, ext2,
    in_sem, send_sem, recv_sem, halo_send, halo_recv,
):
    dates, strip, cols = red.shape
    half = strip // 2
    tiles = half // TILE
    groups = cols // GROUP
    core = lax.axis_index("dates")
    z = lax.axis_index("rows")
    last = lax.axis_size("rows") - 1
    other = 1 - core
    has = jnp.where(core == 0, z > 0, z < last)
    beyond = jnp.where(core == 0, z - 1, z + 1)
    partner = {"dates": other}
    neighbour = {"rows": beyond, "dates": other}

    def tile_in_half(c, k):
        return jnp.where(c == 0, k, tiles - 1 - k)

    def loads(chunk):
        side = chunk // (tiles * groups)
        owner = jnp.where(side == 0, other, core)
        k = (chunk // groups) % tiles
        row = pl.multiple_of(owner * half + tile_in_half(owner, k) * TILE, TILE)
        col = pl.multiple_of((chunk % groups) * GROUP, GROUP)
        return [
            pltpu.make_async_copy(
                src.at[:, pl.ds(row, TILE), pl.ds(col, GROUP)], dst.at[chunk], in_sem.at[chunk, i]
            )
            for i, (src, dst) in enumerate(((red, in_red), (nir, in_nir), (cloud, in_cloud)))
        ]

    chunks = 2 * tiles * groups

    @pl.loop(0, chunks)
    def _(chunk):
        for copy in loads(chunk):
            copy.start()

    barrier = pltpu.get_barrier_semaphore()
    pl.semaphore_signal(barrier, inc=1, device_id=partner, device_id_type=MESH)

    @pl.when(has)
    def _():
        pl.semaphore_signal(barrier, inc=1, device_id=neighbour, device_id_type=MESH)

    shape = (WINDOW, SPAN)
    tap = lax.broadcasted_iota(jnp.int32, shape, 0) - 2 * lax.broadcasted_iota(jnp.int32, shape, 1) - 126
    factor = jnp.zeros(shape, jnp.float32)
    for i, weight in enumerate(TAPS):
        factor = jnp.where(tap == i, weight, factor)
    weights[...] = factor.astype(jnp.bfloat16)
    for buffer in (level, level1, level2):
        rows, width = buffer.shape
        buffer[:, 0:128] = jnp.zeros((rows, 128), jnp.float32)
        buffer[:, width - 128 :] = jnp.zeros((rows, 128), jnp.float32)
    lanes = ext.shape[0]
    ext[:, 0:8] = jnp.zeros((lanes, 8, 128), jnp.float32)
    ext[:, 56:64] = jnp.zeros((lanes, 8, 128), jnp.float32)

    @pl.when(jnp.logical_not(has))
    def _():
        edge = pl.multiple_of(jnp.where(core == 0, 8, 40), 8)
        ext[:, pl.ds(edge, half)] = jnp.zeros((lanes, half, 128), jnp.float32)

    def entry(chunk, d):
        m1, m0 = split(in_nir[chunk, d])
        s1, s0 = split(in_red[chunk, d])
        fresh = jnp.where(in_cloud[chunk, d] == 0, CLEAR, 0)
        return m1, m0, s1, s0, fresh, jnp.full((TILE, GROUP), ordinal[d], jnp.int32)

    def exchange(item):
        return pltpu.make_async_remote_copy(
            src_ref=sent.at[item],
            dst_ref=got.at[item],
            send_sem=send_sem.at[item],
            recv_sem=recv_sem.at[item],
            device_id=partner,
            device_id_type=MESH,
        )

    pl.semaphore_wait(barrier, jnp.where(has, 2, 1))

    @pl.loop(0, tiles * groups)
    def _(item):
        for copy in loads(item):
            copy.wait()
        best = entry(item, 0)
        for d in range(1, dates):
            best = improve(best, entry(item, d))
        n1, n0, r1, r0, clear, order = best
        sent[item, 0] = join(r1, r0)
        sent[item, 1] = join(n1, n0)
        sent[item, 2] = order + jnp.where(clear > 0, FLAG_STEP, 0)
        exchange(item).start()

    def halo(k, side):
        here = tile_in_half(core, k) * TILE
        there = 8 + 32 * (core if side == 0 else other) + here
        return pltpu.make_async_remote_copy(
            src_ref=ext.at[:, pl.ds(pl.multiple_of(24 + here, 8), TILE)],
            dst_ref=ext.at[:, pl.ds(pl.multiple_of(there, 8), TILE)],
            send_sem=halo_send.at[side, k],
            recv_sem=halo_recv.at[side, k],
            device_id=partner if side == 0 else neighbour,
            device_id_type=MESH,
        )

    @pl.loop(0, tiles)
    def _(k):
        row = pl.multiple_of(tile_in_half(core, k) * TILE, TILE)

        @pl.loop(0, groups)
        def _(g):
            item = k * groups + g
            chunk = tiles * groups + item
            for copy in loads(chunk):
                copy.wait()
            exchange(item).wait_recv()
            flagged = got[item, 2]
            is_clear = flagged >= FLAG_STEP
            best = (
                *split(got[item, 1]),
                *split(got[item, 0]),
                jnp.where(is_clear, CLEAR, 0),
                jnp.where(is_clear, flagged - FLAG_STEP, flagged),
            )
            for d in range(dates):
                best = improve(best, entry(chunk, d))
            n1, n0, r1, r0, _, order = best
            value_red, value_nir = join(r1, r0), join(n1, n0)
            col = pl.multiple_of(g * GROUP, GROUP)
            comp_red[pl.ds(row, TILE), pl.ds(col, GROUP)] = value_red
            comp_nir[pl.ds(row, TILE), pl.ds(col, GROUP)] = value_nir
            chosen[pl.ds(row, TILE), pl.ds(col, GROUP)] = order
            inner = pl.ds(pl.multiple_of(col + 128, 128), GROUP)
            level[0:8, inner] = value_red.astype(jnp.float32) * SCALE_BAND
            level[8:16, inner] = value_nir.astype(jnp.float32) * SCALE_BAND

        spans = cols // 2 // SPAN
        results = pooled([level[:, 2 * SPAN * b : 2 * SPAN * b + WINDOW] for b in range(spans)], weights[...])
        mine = pl.ds(pl.multiple_of(24 + row, 8), TILE)
        for b, result in enumerate(results):
            for i in range(SPAN // 128):
                piece = slice(i * 128, (i + 1) * 128)
                ext[b * (SPAN // 128) + i, mine] = result[0:8, piece]
                ext[lanes // 2 + b * (SPAN // 128) + i, mine] = result[8:16, piece]
        halo(k, 0).start()

        @pl.when(has)
        def _():
            halo(k, 1).start()

    for k in range(tiles):
        halo(k, 0).wait_recv()

    @pl.when(has)
    def _():
        for k in range(tiles):
            halo(k, 1).wait_recv()

    def inside(rows, near):
        index = lax.broadcasted_iota(jnp.int32, (rows, 128), 0)
        low = jnp.where(has | (core == 1), 0, near)
        high = jnp.where(has | (core == 0), rows, rows - near)
        return (index >= low) & (index < high)

    def stacked(source, block, start, rows):
        value = TAPS[0] * source[block, pl.ds(start, rows, 2), :]
        for i in range(1, 6):
            value = value + TAPS[i] * source[block, pl.ds(start + i, rows, 2), :]
        return value

    def descend(source, start, rows, keep, near, out, padded, target):
        valid = inside(rows, near)
        blocks = source.shape[0] // 2
        for band in range(2):
            for c in range(blocks):
                value = stacked(source, band * blocks + c, start, rows)
                out[band, :, c * 128 : (c + 1) * 128] = value[keep : keep + out.shape[1]]
                padded[band * rows : (band + 1) * rows, 128 * (c + 1) : 128 * (c + 2)] = jnp.where(valid, value, 0.0)
        spans = blocks * 64 // SPAN
        results = pooled([padded[:, 2 * SPAN * b : 2 * SPAN * b + WINDOW] for b in range(spans)], weights[...])
        for b, result in enumerate(results):
            for band in range(2):
                for i in range(SPAN // 128):
                    target[band * blocks // 2 + b * (SPAN // 128) + i] = result[
                        band * rows : (band + 1) * rows, i * 128 : (i + 1) * 128
                    ]

    descend(ext, 6, 24, 8, 8, one, level1, ext1)
    descend(ext1, 2, 8, 2, 2, two, level2, ext2)
    blocks = ext2.shape[0] // 2
    for band in range(2):
        for c in range(blocks):
            three[band, :, c * 128 : (c + 1) * 128] = stacked(ext2, band * blocks + c, 0, 2)

    @pl.loop(0, tiles * groups)
    def _(item):
        exchange(item).wait_send()

    for k in range(tiles):
        halo(k, 0).wait_send()

    @pl.when(has)
    def _():
        for k in range(tiles):
            halo(k, 1).wait_send()


def body(red_band, nir_band, cloud_class, date_ordinal):
    dates, strip, cols = red_band.shape
    half = strip // 2
    items = half // TILE * (cols // GROUP)
    whole = pl.BlockSpec(memory_space=pltpu.VMEM)
    far = pl.BlockSpec(memory_space=pltpu.HBM)
    f32, i32 = jnp.float32, jnp.int32
    return pl.pallas_call(
        kernel,
        out_shape=[jax.ShapeDtypeStruct((half, cols), i32)] * 3
        + [jax.ShapeDtypeStruct((2, half >> k, cols >> k), f32) for k in (1, 2, 3)],
        in_specs=[pl.BlockSpec(memory_space=pltpu.SMEM), far, far, far],
        out_specs=[whole] * 6,
        scratch_shapes=[pltpu.VMEM((2 * items, dates, TILE, GROUP), i32)] * 3
        + [
            pltpu.VMEM((items, 3, TILE, GROUP), i32),
            pltpu.VMEM((items, 3, TILE, GROUP), i32),
            pltpu.VMEM((16, cols + 256), f32),
            pltpu.VMEM((cols // 128, 64, 128), f32),
            pltpu.VMEM((WINDOW, SPAN), jnp.bfloat16),
            pltpu.VMEM((48, cols // 2 + 256), f32),
            pltpu.VMEM((cols // 256, 24, 128), f32),
            pltpu.VMEM((16, cols // 4 + 256), f32),
            pltpu.VMEM((cols // 512, 8, 128), f32),
            pltpu.SemaphoreType.DMA((2 * items, 3)),
            pltpu.SemaphoreType.DMA((items,)),
            pltpu.SemaphoreType.DMA((items,)),
            pltpu.SemaphoreType.DMA((2, half // TILE)),
            pltpu.SemaphoreType.DMA((2, half // TILE)),
        ],
        compiler_params=pltpu.CompilerParams(collective_id=0, has_side_effects=True),
        name="composite",
    )(date_ordinal, red_band, nir_band, cloud_class)


def solution(mesh):
    in_specs = (
        P("dates", ("tiles", "rows"), None),
        P("dates", ("tiles", "rows"), None),
        P("dates", ("tiles", "rows"), None),
        P(("tiles", "dates")),
    )
    out_specs = (
        P(("tiles", "rows", "dates"), None),
        P(("tiles", "rows", "dates"), None),
        P(("tiles", "rows", "dates"), None),
        P(None, ("tiles", "rows", "dates"), None),
        P(None, ("tiles", "rows", "dates"), None),
        P(None, ("tiles", "rows", "dates"), None),
    )
    return jax.shard_map(body, mesh=mesh, in_specs=in_specs, out_specs=out_specs, check_vma=False)
```

time: 210 us -> 39.7 us (0.19)
  other arithmetic: 91 us -> 0 us
  local copies, waits for them, and re-layouts: 47.5 us -> 8.77 us
  Pallas kernels: 0 us -> 30 us
  blocking collectives: 26.7 us -> 0 us
  loops' own time: 21.6 us -> 0 us
  starting transfers between devices: 13.3 us -> 0 us
  waiting for transfers between devices: 7.84 us -> 0 us
    select_n x22 -> x0, other arithmetic: 71.4 us -> none  [better(): return tuple((jnp.where(take, one, two) for one, two in zip(first, second)))]
    pallas_call x0 -> x1, Pallas kernels: none -> 30 us  [body(): pl.pallas_call(kernel, out_shape=[jax.ShapeDtypeStruct((half, cols), i32)...]
    all_gather x3 -> x0, blocking collectives: 26.7 us -> none  [merged_2(): pieces = jax.tree.map(lambda part: lax.all_gather(part, axis), value)]
    reshape x3 -> x0, local copies, waits for them, and re-layouts: 25.5 us -> none  [smooth_pool(): return result.reshape(2, rows // 2, 2, cols // 2, 2).mean(axis=(2, 4))]
    another operation x1 -> x0, loops' own time: 21.6 us -> none  [body(): lax.scan(advance, entry(0), jnp.arange(1, red_band.shape[0], dtype=jnp.in...]
    dynamic_slice x22 -> x0, local copies, waits for them, and re-layouts: 20.1 us -> none  [the longest x11 13.7 us: entry(): date_ordinal[index]]
    ppermute x6 -> x0, starting transfers between devices: 13.3 us -> none  [the longest x3 7.47 us: extended(): lax.ppermute(first, axis, [(b, a) for a, b in up])]
    reduce_sum x3 -> x0, other arithmetic: 11 us -> none  [smooth_pool(): return result.reshape(2, rows // 2, 2, cols // 2, 2).mean(axis=(2, 4))]
  transfers between devices with their start and end apart: 6 -> 0, of which waited for: 3 -> 0; matrix products, arithmetic and copies ran while one was open for 0% -> 0% of each run, Pallas kernels for 0% -> 0%
where the time goes in v1:
time: 39.7 us; the launch traced here: 39.4 us
  Pallas kernels  30 us (76%)
  local copies, waits for them, and re-layouts  8.77 us (22%)
  between operations  0.64 us (2%)
    pallas_call x1, Pallas kernels, body(): pl.pallas_call(kernel, out_shape=[jax.ShapeDtypeStruct((half, cols), i32)...  30 us
    unnamed x6, local copies, waits for them, and re-layouts  8.77 us

profile of v1, /device:TPU:37, one launch (start us, length us, event | category | flops | bytes accessed | tf_op | source)
XLA Modules:
  0.0 39.4 jit_solution(14472049219609404759)
XLA Ops:
  0.6 30.0 %composite.1 = (s32[16,2048]{1,0:T(8,128)}, s32[16,2048]{1,0:T(8,128)}, s32[16,2048]{1,0:T(8,128)}, f32[2,8,1024]{2,1,0:T(8,128)}, f32[2,4,512]{2,1,0:T(4,128)}, /*index=5*/f32[2,2,256]{2,1,0:T(2,128)}) custom-call(s32[12]{0:T(128)} %ordinal.1, s32[12,32,2048]{2,1,0:T(8,128)} %red.1, s32[12,32,2048]{2,1,0:T(8,128)} %nir.1, s32[12,32,2048]{2,1,0:T(8,128)} %cloud.1), custom_call_target="tpu_custom_call" | custom-call | tf_op jit(solution)/shard_map/composite/pallas_call | solution.py:271
  30.6 1.6 %copy.16 = s32[16,2048]{1,0:T(8,128)} copy(s32[16,2048]{1,0:T(8,128)} %get-tuple-element.12) | data formatting | bytes 262144
  32.2 1.6 %copy.17 = s32[16,2048]{1,0:T(8,128)} copy(s32[16,2048]{1,0:T(8,128)} %get-tuple-element.13) | data formatting | bytes 262144
  33.8 1.6 %copy.18 = s32[16,2048]{1,0:T(8,128)} copy(s32[16,2048]{1,0:T(8,128)} %get-tuple-element.14) | data formatting | bytes 262144
  35.3 1.5 %copy.19 = f32[2,8,1024]{2,1,0:T(8,128)} copy(f32[2,8,1024]{2,1,0:T(8,128)} %get-tuple-element.15) | data formatting | bytes 131072
  36.8 1.3 %copy.20 = f32[2,4,512]{2,1,0:T(4,128)} copy(f32[2,4,512]{2,1,0:T(4,128)} %get-tuple-element.16) | data formatting | bytes 32768
  38.1 1.3 %copy.21 = f32[2,2,256]{2,1,0:T(2,128)} copy(f32[2,2,256]{2,1,0:T(2,128)} %get-tuple-element.17) | data formatting | bytes 8192

commit v2 on v1

--- a/solution.py
+++ b/solution.py
@@ -38,6 +38,12 @@
     return tuple(jnp.where(take, one, two) for one, two in zip(new, best))
 
 
+def clear_margins(buffer):
+    rows, width = buffer.shape
+    buffer[:, 0:128] = jnp.zeros((rows, 128), jnp.float32)
+    buffer[:, width - 128 :] = jnp.zeros((rows, 128), jnp.float32)
+
+
 def pooled(window, weights):
     parts = []
     for block in window:
@@ -49,10 +55,10 @@
 
 
 def kernel(
-    ordinal, red, nir, cloud,
-    comp_red, comp_nir, chosen, one, two, three,
-    in_red, in_nir, in_cloud, sent, got, level, ext, weights, level1, ext1, level2, ext2,
-    in_sem, send_sem, recv_sem, halo_send, halo_recv,
+    ordinal_far, red, nir, cloud,
+    comp_red, comp_nir, chosen, ext, weights,
+    ordinal, in_red, in_nir, in_cloud, sent, got, level,
+    in_sem, ordinal_sem, send_sem, recv_sem, halo_send, halo_recv,
 ):
     dates, strip, cols = red.shape
     half = strip // 2
@@ -90,6 +96,8 @@
         for copy in loads(chunk):
             copy.start()
 
+    order_copy = pltpu.make_async_copy(ordinal_far, ordinal, ordinal_sem)
+    order_copy.start()
     barrier = pltpu.get_barrier_semaphore()
     pl.semaphore_signal(barrier, inc=1, device_id=partner, device_id_type=MESH)
 
@@ -103,10 +111,7 @@
     for i, weight in enumerate(TAPS):
         factor = jnp.where(tap == i, weight, factor)
     weights[...] = factor.astype(jnp.bfloat16)
-    for buffer in (level, level1, level2):
-        rows, width = buffer.shape
-        buffer[:, 0:128] = jnp.zeros((rows, 128), jnp.float32)
-        buffer[:, width - 128 :] = jnp.zeros((rows, 128), jnp.float32)
+    clear_margins(level)
     lanes = ext.shape[0]
     ext[:, 0:8] = jnp.zeros((lanes, 8, 128), jnp.float32)
     ext[:, 56:64] = jnp.zeros((lanes, 8, 128), jnp.float32)
@@ -132,6 +137,7 @@
             device_id_type=MESH,
         )
 
+    order_copy.wait()
     pl.semaphore_wait(barrier, jnp.where(has, 2, 1))
 
     @pl.loop(0, tiles * groups)
@@ -212,6 +218,34 @@
         for k in range(tiles):
             halo(k, 1).wait_recv()
 
+    @pl.loop(0, tiles * groups)
+    def _(item):
+        exchange(item).wait_send()
+
+    for k in range(tiles):
+        halo(k, 0).wait_send()
+
+    @pl.when(has)
+    def _():
+        for k in range(tiles):
+            halo(k, 1).wait_send()
+
+
+def finish(
+    comp_red, comp_nir, chosen, ext, weights,
+    out_red, out_nir, out_chosen, out_one, out_two, out_three,
+    level1, ext1, level2, ext2, one, two, three, sems,
+):
+    pairs = ((comp_red, out_red), (comp_nir, out_nir), (chosen, out_chosen), (one, out_one), (two, out_two), (three, out_three))
+    copies = [pltpu.make_async_copy(src, dst, sems.at[i]) for i, (src, dst) in enumerate(pairs)]
+    for copy in copies[:3]:
+        copy.start()
+    core = lax.axis_index("dates")
+    z = lax.axis_index("rows")
+    has = jnp.where(core == 0, z > 0, z < lax.axis_size("rows") - 1)
+    clear_margins(level1)
+    clear_margins(level2)
+
     def inside(rows, near):
         index = lax.broadcasted_iota(jnp.int32, (rows, 128), 0)
         low = jnp.where(has | (core == 1), 0, near)
@@ -242,23 +276,17 @@
                     ]
 
     descend(ext, 6, 24, 8, 8, one, level1, ext1)
+    copies[3].start()
     descend(ext1, 2, 8, 2, 2, two, level2, ext2)
+    copies[4].start()
     blocks = ext2.shape[0] // 2
     for band in range(2):
         for c in range(blocks):
             three[band, :, c * 128 : (c + 1) * 128] = stacked(ext2, band * blocks + c, 0, 2)
 
-    @pl.loop(0, tiles * groups)
-    def _(item):
-        exchange(item).wait_send()
-
-    for k in range(tiles):
-        halo(k, 0).wait_send()
-
-    @pl.when(has)
-    def _():
-        for k in range(tiles):
-            halo(k, 1).wait_send()
+    copies[5].start()
+    for copy in copies:
+        copy.wait()
 
 
 def body(red_band, nir_band, cloud_class, date_ordinal):
@@ -268,32 +296,49 @@
     whole = pl.BlockSpec(memory_space=pltpu.VMEM)
     far = pl.BlockSpec(memory_space=pltpu.HBM)
     f32, i32 = jnp.float32, jnp.int32
-    return pl.pallas_call(
+    arrays = (date_ordinal, red_band, nir_band, cloud_class)
+    arrays = [pltpu.with_memory_space_constraint(array, pltpu.HBM) for array in arrays]
+    near = pl.pallas_call(
         kernel,
-        out_shape=[jax.ShapeDtypeStruct((half, cols), i32)] * 3
-        + [jax.ShapeDtypeStruct((2, half >> k, cols >> k), f32) for k in (1, 2, 3)],
-        in_specs=[pl.BlockSpec(memory_space=pltpu.SMEM), far, far, far],
-        out_specs=[whole] * 6,
-        scratch_shapes=[pltpu.VMEM((2 * items, dates, TILE, GROUP), i32)] * 3
+        out_shape=[pltpu.VMEM((half, cols), i32)] * 3
+        + [pltpu.VMEM((cols // 128, 64, 128), f32), pltpu.VMEM((WINDOW, SPAN), jnp.bfloat16)],
+        in_specs=[far] * 4,
+        out_specs=[whole] * 5,
+        scratch_shapes=[pltpu.SMEM((dates,), i32)]
+        + [pltpu.VMEM((2 * items, dates, TILE, GROUP), i32)] * 3
         + [
             pltpu.VMEM((items, 3, TILE, GROUP), i32),
             pltpu.VMEM((items, 3, TILE, GROUP), i32),
             pltpu.VMEM((16, cols + 256), f32),
-            pltpu.VMEM((cols // 128, 64, 128), f32),
-            pltpu.VMEM((WINDOW, SPAN), jnp.bfloat16),
-            pltpu.VMEM((48, cols // 2 + 256), f32),
-            pltpu.VMEM((cols // 256, 24, 128), f32),
-            pltpu.VMEM((16, cols // 4 + 256), f32),
-            pltpu.VMEM((cols // 512, 8, 128), f32),
             pltpu.SemaphoreType.DMA((2 * items, 3)),
+            pltpu.SemaphoreType.DMA,
             pltpu.SemaphoreType.DMA((items,)),
             pltpu.SemaphoreType.DMA((items,)),
             pltpu.SemaphoreType.DMA((2, half // TILE)),
             pltpu.SemaphoreType.DMA((2, half // TILE)),
         ],
-        compiler_params=pltpu.CompilerParams(collective_id=0, has_side_effects=True),
+        compiler_params=pltpu.CompilerParams(
+            collective_id=0, has_side_effects=True, vmem_limit_bytes=32 * 1024 * 1024
+        ),
         name="composite",
-    )(date_ordinal, red_band, nir_band, cloud_class)
+    )(*arrays)
+    levels = [(2, half >> k, cols >> k) for k in (1, 2, 3)]
+    return pl.pallas_call(
+        finish,
+        out_shape=[jax.ShapeDtypeStruct((half, cols), i32)] * 3 + [jax.ShapeDtypeStruct(shape, f32) for shape in levels],
+        in_specs=[whole] * 5,
+        out_specs=[far] * 6,
+        scratch_shapes=[
+            pltpu.VMEM((48, cols // 2 + 256), f32),
+            pltpu.VMEM((cols // 256, 24, 128), f32),
+            pltpu.VMEM((16, cols // 4 + 256), f32),
+            pltpu.VMEM((cols // 512, 8, 128), f32),
+        ]
+        + [pltpu.VMEM(shape, f32) for shape in levels]
+        + [pltpu.SemaphoreType.DMA((6,))],
+        compiler_params=pltpu.CompilerParams(vmem_limit_bytes=16 * 1024 * 1024),
+        name="finish",
+    )(*near)
 
 
 def solution(mesh):

time: 39.7 us -> 30 us (0.76)
  local copies, waits for them, and re-layouts: 8.77 us -> 0 us
  Pallas kernels: 30 us -> 29.3 us
    unnamed x6 -> x0, local copies, waits for them, and re-layouts: 8.77 us -> none
    pallas_call x1 -> x2, Pallas kernels: 30 us -> 29.3 us  [the longest x1 28.1 us: body(): pl.pallas_call(kernel, out_shape=[pltpu.VMEM((half, cols), i32)] * 3 + [p...]
where the time goes in v2:
time: 30 us; the launch traced here: 29.9 us
  Pallas kernels  29.3 us (98%)
  between operations  0.64 us (2%)
    pallas_call x1, Pallas kernels, body(): pl.pallas_call(kernel, out_shape=[pltpu.VMEM((half, cols), i32)] * 3 + [p...  28.1 us
    pallas_call x1, Pallas kernels, body(): pl.pallas_call(finish, out_shape=[jax.ShapeDtypeStruct((half, cols), i32)...  1.14 us

profile of v2, /device:TPU:37, one launch (start us, length us, event | category | flops | bytes accessed | tf_op | source)
XLA Modules:
  0.0 29.9 jit_solution(4531462365789908704)
XLA Ops:
  0.6 28.1 %composite.1 = (s32[16,2048]{1,0:T(8,128)S(1)}, s32[16,2048]{1,0:T(8,128)S(1)}, s32[16,2048]{1,0:T(8,128)S(1)}, f32[16,64,128]{2,1,0:T(8,128)S(1)}, bf16[768,256]{1,0:T(8,128)(2,1)S(1)}) custom-call(s32[12]{0:T(128)} %ordinal_far.1, s32[12,32,2048]{2,1,0:T(8,128)} %red.1, s32[12,32,2048]{2,1,0:T(8,128)} %nir.1, s32[12,32,2048]{2,1,0:T(8,128)} %cloud.1), custom_call_target="tpu_custom_call" | custom-call | tf_op jit(solution)/shard_map/composite/pallas_call | solution.py:301
  28.8 1.1 %finish.1 = (s32[16,2048]{1,0:T(8,128)}, s32[16,2048]{1,0:T(8,128)}, s32[16,2048]{1,0:T(8,128)}, f32[2,8,1024]{2,1,0:T(8,128)}, f32[2,4,512]{2,1,0:T(4,128)}, /*index=5*/f32[2,2,256]{2,1,0:T(2,128)}) custom-call(s32[16,2048]{1,0:T(8,128)S(1)} %get-tuple-element.11.comp_red, s32[16,2048]{1,0:T(8,128)S(1)} %get-tuple-element.12.comp_nir, ...), custom_call_target="tpu_custom_call" | custom-call | tf_op jit(solution)/shard_map/finish/pallas_call | solution.py:326

commit v3 on v2

--- a/solution.py
+++ b/solution.py
@@ -16,6 +16,7 @@
 TAPS = (0.03125, 0.15625, 0.3125, 0.3125, 0.15625, 0.03125)
 TILE = 8
 GROUP = 512
+PART = 1024
 SPAN = 256
 WINDOW = 2 * SPAN + 256
 
@@ -33,8 +34,8 @@
     m1, m0, s1, s0, fresh, index = new
     low = m0 * r0 - n0 * s0 + ((order - index) >> 31)
     mid = (m1 * r0 + m0 * r1) - (n1 * s0 + n0 * s1) + (low >> LIMB_BITS)
-    top = m1 * r1 - n1 * s1 + (mid >> LIMB_BITS) + (fresh - clear)
-    take = top >= 0
+    top = m1 * r1 - n1 * s1 + (mid >> LIMB_BITS)
+    take = top >= clear - fresh
     return tuple(jnp.where(take, one, two) for one, two in zip(new, best))
 
 
@@ -63,7 +64,6 @@
     dates, strip, cols = red.shape
     half = strip // 2
     tiles = half // TILE
-    groups = cols // GROUP
     core = lax.axis_index("dates")
     z = lax.axis_index("rows")
     last = lax.axis_size("rows") - 1
@@ -76,28 +76,23 @@
     def tile_in_half(c, k):
         return jnp.where(c == 0, k, tiles - 1 - k)
 
-    def loads(chunk):
-        side = chunk // (tiles * groups)
-        owner = jnp.where(side == 0, other, core)
-        k = (chunk // groups) % tiles
-        row = pl.multiple_of(owner * half + tile_in_half(owner, k) * TILE, TILE)
-        col = pl.multiple_of((chunk % groups) * GROUP, GROUP)
+    def load(slot, part):
+        owner = jnp.where(slot < tiles, other, core)
+        row = pl.multiple_of(owner * half + tile_in_half(owner, slot % tiles) * TILE, TILE)
+        col = pl.ds(part * PART, PART)
         return [
-            pltpu.make_async_copy(
-                src.at[:, pl.ds(row, TILE), pl.ds(col, GROUP)], dst.at[chunk], in_sem.at[chunk, i]
-            )
+            pltpu.make_async_copy(src.at[:, pl.ds(row, TILE), col], dst.at[slot, :, :, col], in_sem.at[slot, part, i])
             for i, (src, dst) in enumerate(((red, in_red), (nir, in_nir), (cloud, in_cloud)))
         ]
 
-    chunks = 2 * tiles * groups
-
-    @pl.loop(0, chunks)
-    def _(chunk):
-        for copy in loads(chunk):
-            copy.start()
-
+    parts = cols // PART
     order_copy = pltpu.make_async_copy(ordinal_far, ordinal, ordinal_sem)
     order_copy.start()
+    for slot in range(2 * tiles):
+        for part in range(parts):
+            for copy in load(slot, part):
+                copy.start()
+
     barrier = pltpu.get_barrier_semaphore()
     pl.semaphore_signal(barrier, inc=1, device_id=partner, device_id_type=MESH)
 
@@ -121,37 +116,49 @@
         edge = pl.multiple_of(jnp.where(core == 0, 8, 40), 8)
         ext[:, pl.ds(edge, half)] = jnp.zeros((lanes, half, 128), jnp.float32)
 
-    def entry(chunk, d):
-        m1, m0 = split(in_nir[chunk, d])
-        s1, s0 = split(in_red[chunk, d])
-        fresh = jnp.where(in_cloud[chunk, d] == 0, CLEAR, 0)
+    def entry(slot, d, col):
+        m1, m0 = split(in_nir[slot, d, :, col])
+        s1, s0 = split(in_red[slot, d, :, col])
+        fresh = jnp.where(in_cloud[slot, d, :, col] == 0, CLEAR, 0)
         return m1, m0, s1, s0, fresh, jnp.full((TILE, GROUP), ordinal[d], jnp.int32)
 
-    def exchange(item):
+    def exchange(k):
         return pltpu.make_async_remote_copy(
-            src_ref=sent.at[item],
-            dst_ref=got.at[item],
-            send_sem=send_sem.at[item],
-            recv_sem=recv_sem.at[item],
+            src_ref=sent.at[k],
+            dst_ref=got.at[k],
+            send_sem=send_sem.at[k],
+            recv_sem=recv_sem.at[k],
             device_id=partner,
             device_id_type=MESH,
         )
 
+    def offer(slot, col):
+        best = entry(slot, 0, col)
+        for d in range(1, dates):
+            best = improve(best, entry(slot, d, col))
+        n1, n0, r1, r0, clear, order = best
+        sent[slot, 0, :, col] = join(r1, r0)
+        sent[slot, 1, :, col] = join(n1, n0)
+        sent[slot, 2, :, col] = order + jnp.where(clear > 0, FLAG_STEP, 0)
+
+    def columns(start, count):
+        return [pl.ds(start + i * GROUP, GROUP) for i in range(count // GROUP)]
+
     order_copy.wait()
+    for part in range(parts):
+        for copy in load(0, part):
+            copy.wait()
+        for col in columns(part * PART, PART):
+            offer(0, col)
     pl.semaphore_wait(barrier, jnp.where(has, 2, 1))
-
-    @pl.loop(0, tiles * groups)
-    def _(item):
-        for copy in loads(item):
-            copy.wait()
-        best = entry(item, 0)
-        for d in range(1, dates):
-            best = improve(best, entry(item, d))
-        n1, n0, r1, r0, clear, order = best
-        sent[item, 0] = join(r1, r0)
-        sent[item, 1] = join(n1, n0)
-        sent[item, 2] = order + jnp.where(clear > 0, FLAG_STEP, 0)
-        exchange(item).start()
+    exchange(0).start()
+    for slot in range(1, tiles):
+        for part in range(parts):
+            for copy in load(slot, part):
+                copy.wait()
+        for col in columns(0, cols):
+            offer(slot, col)
+        exchange(slot).start()
 
     def halo(k, side):
         here = tile_in_half(core, k) * TILE
@@ -168,31 +175,28 @@
     @pl.loop(0, tiles)
     def _(k):
         row = pl.multiple_of(tile_in_half(core, k) * TILE, TILE)
-
-        @pl.loop(0, groups)
-        def _(g):
-            item = k * groups + g
-            chunk = tiles * groups + item
-            for copy in loads(chunk):
+        slot = tiles + k
+        for part in range(parts):
+            for copy in load(slot, part):
                 copy.wait()
-            exchange(item).wait_recv()
-            flagged = got[item, 2]
+        exchange(k).wait_recv()
+        for col in columns(0, cols):
+            flagged = got[k, 2, :, col]
             is_clear = flagged >= FLAG_STEP
             best = (
-                *split(got[item, 1]),
-                *split(got[item, 0]),
+                *split(got[k, 1, :, col]),
+                *split(got[k, 0, :, col]),
                 jnp.where(is_clear, CLEAR, 0),
                 jnp.where(is_clear, flagged - FLAG_STEP, flagged),
             )
             for d in range(dates):
-                best = improve(best, entry(chunk, d))
+                best = improve(best, entry(slot, d, col))
             n1, n0, r1, r0, _, order = best
             value_red, value_nir = join(r1, r0), join(n1, n0)
-            col = pl.multiple_of(g * GROUP, GROUP)
-            comp_red[pl.ds(row, TILE), pl.ds(col, GROUP)] = value_red
-            comp_nir[pl.ds(row, TILE), pl.ds(col, GROUP)] = value_nir
-            chosen[pl.ds(row, TILE), pl.ds(col, GROUP)] = order
-            inner = pl.ds(pl.multiple_of(col + 128, 128), GROUP)
+            comp_red[pl.ds(row, TILE), col] = value_red
+            comp_nir[pl.ds(row, TILE), col] = value_nir
+            chosen[pl.ds(row, TILE), col] = order
+            inner = pl.ds(col.start + 128, GROUP)
             level[0:8, inner] = value_red.astype(jnp.float32) * SCALE_BAND
             level[8:16, inner] = value_nir.astype(jnp.float32) * SCALE_BAND
 
@@ -218,11 +222,8 @@
         for k in range(tiles):
             halo(k, 1).wait_recv()
 
-    @pl.loop(0, tiles * groups)
-    def _(item):
-        exchange(item).wait_send()
-
     for k in range(tiles):
+        exchange(k).wait_send()
         halo(k, 0).wait_send()
 
     @pl.when(has)
@@ -292,7 +293,7 @@
 def body(red_band, nir_band, cloud_class, date_ordinal):
     dates, strip, cols = red_band.shape
     half = strip // 2
-    items = half // TILE * (cols // GROUP)
+    tiles = half // TILE
     whole = pl.BlockSpec(memory_space=pltpu.VMEM)
     far = pl.BlockSpec(memory_space=pltpu.HBM)
     f32, i32 = jnp.float32, jnp.int32
@@ -305,17 +306,17 @@
         in_specs=[far] * 4,
         out_specs=[whole] * 5,
         scratch_shapes=[pltpu.SMEM((dates,), i32)]
-        + [pltpu.VMEM((2 * items, dates, TILE, GROUP), i32)] * 3
+        + [pltpu.VMEM((2 * tiles, dates, TILE, cols), i32)] * 3
         + [
-            pltpu.VMEM((items, 3, TILE, GROUP), i32),
-            pltpu.VMEM((items, 3, TILE, GROUP), i32),
+            pltpu.VMEM((tiles, 3, TILE, cols), i32),
+            pltpu.VMEM((tiles, 3, TILE, cols), i32),
             pltpu.VMEM((16, cols + 256), f32),
-            pltpu.SemaphoreType.DMA((2 * items, 3)),
+            pltpu.SemaphoreType.DMA((2 * tiles, cols // PART, 3)),
             pltpu.SemaphoreType.DMA,
-            pltpu.SemaphoreType.DMA((items,)),
-            pltpu.SemaphoreType.DMA((items,)),
-            pltpu.SemaphoreType.DMA((2, half // TILE)),
-            pltpu.SemaphoreType.DMA((2, half // TILE)),
+            pltpu.SemaphoreType.DMA((tiles,)),
+            pltpu.SemaphoreType.DMA((tiles,)),
+            pltpu.SemaphoreType.DMA((2, tiles)),
+            pltpu.SemaphoreType.DMA((2, tiles)),
         ],
         compiler_params=pltpu.CompilerParams(
             collective_id=0, has_side_effects=True, vmem_limit_bytes=32 * 1024 * 1024

time: 30 us -> 29.4 us (0.980)
  Pallas kernels: 29.3 us -> 28.7 us
    pallas_call x1, Pallas kernels: 28.1 us -> 27.5 us  [body(): pl.pallas_call(kernel, out_shape=[pltpu.VMEM((half, cols), i32)] * 3 + [p...]
where the time goes in v3:
time: 29.4 us; the launch traced here: 29.3 us
  Pallas kernels  28.7 us (98%)
  between operations  0.64 us (2%)
    pallas_call x1, Pallas kernels, body(): pl.pallas_call(kernel, out_shape=[pltpu.VMEM((half, cols), i32)] * 3 + [p...  27.5 us
    pallas_call x1, Pallas kernels, body(): pl.pallas_call(finish, out_shape=[jax.ShapeDtypeStruct((half, cols), i32)...  1.14 us

profile of v3, /device:TPU:37, one launch (start us, length us, event | category | flops | bytes accessed | tf_op | source)
XLA Modules:
  0.0 29.3 jit_solution(13718238528545116175)
XLA Ops:
  0.6 27.5 %composite.1 = (s32[16,2048]{1,0:T(8,128)S(1)}, s32[16,2048]{1,0:T(8,128)S(1)}, s32[16,2048]{1,0:T(8,128)S(1)}, f32[16,64,128]{2,1,0:T(8,128)S(1)}, bf16[768,256]{1,0:T(8,128)(2,1)S(1)}) custom-call(s32[12]{0:T(128)} %ordinal_far.1, s32[12,32,2048]{2,1,0:T(8,128)} %red.1, s32[12,32,2048]{2,1,0:T(8,128)} %nir.1, s32[12,32,2048]{2,1,0:T(8,128)} %cloud.1), custom_call_target="tpu_custom_call" | custom-call | tf_op jit(solution)/shard_map/composite/pallas_call | solution.py:302
  28.2 1.1 %finish.1 = (s32[16,2048]{1,0:T(8,128)}, s32[16,2048]{1,0:T(8,128)}, s32[16,2048]{1,0:T(8,128)}, f32[2,8,1024]{2,1,0:T(8,128)}, f32[2,4,512]{2,1,0:T(4,128)}, /*index=5*/f32[2,2,256]{2,1,0:T(2,128)}) custom-call(s32[16,2048]{1,0:T(8,128)S(1)} %get-tuple-element.11.comp_red, s32[16,2048]{1,0:T(8,128)S(1)} %get-tuple-element.12.comp_nir, ...), custom_call_target="tpu_custom_call" | custom-call | tf_op jit(solution)/shard_map/finish/pallas_call | solution.py:327

commit v4 on v3

--- a/solution.py
+++ b/solution.py
@@ -57,8 +57,8 @@
 
 def kernel(
     ordinal_far, red, nir, cloud,
-    comp_red, comp_nir, chosen, ext, weights,
-    ordinal, in_red, in_nir, in_cloud, sent, got, level,
+    comp, ext, weights,
+    ordinal, images, sent, got, mine, level,
     in_sem, ordinal_sem, send_sem, recv_sem, halo_send, halo_recv,
 ):
     dates, strip, cols = red.shape
@@ -76,22 +76,25 @@
     def tile_in_half(c, k):
         return jnp.where(c == 0, k, tiles - 1 - k)
 
-    def load(slot, part):
-        owner = jnp.where(slot < tiles, other, core)
+    pieces = [(0, part, PART) for part in range(0, cols, PART)] + [(slot, 0, cols) for slot in range(1, 2 * tiles)]
+
+    def load(i):
+        slot, start, width = pieces[i]
+        owner = other if slot < tiles else core
         row = pl.multiple_of(owner * half + tile_in_half(owner, slot % tiles) * TILE, TILE)
-        col = pl.ds(part * PART, PART)
-        return [
-            pltpu.make_async_copy(src.at[:, pl.ds(row, TILE), col], dst.at[slot, :, :, col], in_sem.at[slot, part, i])
-            for i, (src, dst) in enumerate(((red, in_red), (nir, in_nir), (cloud, in_cloud)))
-        ]
-
-    parts = cols // PART
+        col = pl.ds(start, width)
+        for j, src in enumerate((red, nir, cloud)):
+            pltpu.make_async_copy(src.at[:, pl.ds(row, TILE), col], images.at[slot, j, :, :, col], in_sem.at[i]).start()
+
+    def loaded(i):
+        slot, start, width = pieces[i]
+        there = images.at[slot, :, :, :, pl.ds(start, width)]
+        pltpu.make_async_copy(there, there, in_sem.at[i]).wait()
+
     order_copy = pltpu.make_async_copy(ordinal_far, ordinal, ordinal_sem)
     order_copy.start()
-    for slot in range(2 * tiles):
-        for part in range(parts):
-            for copy in load(slot, part):
-                copy.start()
+    for i in range(len(pieces)):
+        load(i)
 
     barrier = pltpu.get_barrier_semaphore()
     pl.semaphore_signal(barrier, inc=1, device_id=partner, device_id_type=MESH)
@@ -117,48 +120,53 @@
         ext[:, pl.ds(edge, half)] = jnp.zeros((lanes, half, 128), jnp.float32)
 
     def entry(slot, d, col):
-        m1, m0 = split(in_nir[slot, d, :, col])
-        s1, s0 = split(in_red[slot, d, :, col])
-        fresh = jnp.where(in_cloud[slot, d, :, col] == 0, CLEAR, 0)
+        m1, m0 = split(images[slot, 1, d, :, col])
+        s1, s0 = split(images[slot, 0, d, :, col])
+        fresh = jnp.where(images[slot, 2, d, :, col] == 0, CLEAR, 0)
         return m1, m0, s1, s0, fresh, jnp.full((TILE, GROUP), ordinal[d], jnp.int32)
 
     def exchange(k):
         return pltpu.make_async_remote_copy(
             src_ref=sent.at[k],
             dst_ref=got.at[k],
-            send_sem=send_sem.at[k],
+            send_sem=send_sem,
             recv_sem=recv_sem.at[k],
             device_id=partner,
             device_id_type=MESH,
         )
 
-    def offer(slot, col):
+    def columns(start, count):
+        return [pl.ds(start + i * GROUP, GROUP) for i in range(count // GROUP)]
+
+    def best_of(slot, col):
         best = entry(slot, 0, col)
         for d in range(1, dates):
             best = improve(best, entry(slot, d, col))
-        n1, n0, r1, r0, clear, order = best
+        return best
+
+    def offer(slot, col):
+        n1, n0, r1, r0, clear, order = best_of(slot, col)
         sent[slot, 0, :, col] = join(r1, r0)
         sent[slot, 1, :, col] = join(n1, n0)
         sent[slot, 2, :, col] = order + jnp.where(clear > 0, FLAG_STEP, 0)
 
-    def columns(start, count):
-        return [pl.ds(start + i * GROUP, GROUP) for i in range(count // GROUP)]
-
     order_copy.wait()
-    for part in range(parts):
-        for copy in load(0, part):
-            copy.wait()
-        for col in columns(part * PART, PART):
-            offer(0, col)
-    pl.semaphore_wait(barrier, jnp.where(has, 2, 1))
-    exchange(0).start()
-    for slot in range(1, tiles):
-        for part in range(parts):
-            for copy in load(slot, part):
-                copy.wait()
+    for i, (slot, start, width) in enumerate(pieces):
+        if slot < tiles:
+            loaded(i)
+            for col in columns(start, width):
+                offer(slot, col)
+            if start + width == cols:
+                if slot == 0:
+                    pl.semaphore_wait(barrier, jnp.where(has, 2, 1))
+                exchange(slot).start()
+
+    base = len(pieces) - tiles
+    for k in range(tiles):
+        loaded(base + k)
         for col in columns(0, cols):
-            offer(slot, col)
-        exchange(slot).start()
+            for i, limb in enumerate(best_of(tiles + k, col)):
+                mine[k, i, :, col] = limb
 
     def halo(k, side):
         here = tile_in_half(core, k) * TILE
@@ -166,81 +174,77 @@
         return pltpu.make_async_remote_copy(
             src_ref=ext.at[:, pl.ds(pl.multiple_of(24 + here, 8), TILE)],
             dst_ref=ext.at[:, pl.ds(pl.multiple_of(there, 8), TILE)],
-            send_sem=halo_send.at[side, k],
-            recv_sem=halo_recv.at[side, k],
+            send_sem=halo_send.at[side],
+            recv_sem=halo_recv.at[side],
             device_id=partner if side == 0 else neighbour,
             device_id_type=MESH,
         )
 
-    @pl.loop(0, tiles)
-    def _(k):
+    def settle(k):
         row = pl.multiple_of(tile_in_half(core, k) * TILE, TILE)
-        slot = tiles + k
-        for part in range(parts):
-            for copy in load(slot, part):
-                copy.wait()
-        exchange(k).wait_recv()
         for col in columns(0, cols):
             flagged = got[k, 2, :, col]
             is_clear = flagged >= FLAG_STEP
-            best = (
+            theirs = (
                 *split(got[k, 1, :, col]),
                 *split(got[k, 0, :, col]),
                 jnp.where(is_clear, CLEAR, 0),
                 jnp.where(is_clear, flagged - FLAG_STEP, flagged),
             )
-            for d in range(dates):
-                best = improve(best, entry(slot, d, col))
-            n1, n0, r1, r0, _, order = best
+            n1, n0, r1, r0, _, order = improve(tuple(mine[k, i, :, col] for i in range(6)), theirs)
             value_red, value_nir = join(r1, r0), join(n1, n0)
-            comp_red[pl.ds(row, TILE), col] = value_red
-            comp_nir[pl.ds(row, TILE), col] = value_nir
-            chosen[pl.ds(row, TILE), col] = order
+            comp[0, pl.ds(row, TILE), col] = value_red
+            comp[1, pl.ds(row, TILE), col] = value_nir
+            comp[2, pl.ds(row, TILE), col] = order
             inner = pl.ds(col.start + 128, GROUP)
             level[0:8, inner] = value_red.astype(jnp.float32) * SCALE_BAND
             level[8:16, inner] = value_nir.astype(jnp.float32) * SCALE_BAND
 
         spans = cols // 2 // SPAN
         results = pooled([level[:, 2 * SPAN * b : 2 * SPAN * b + WINDOW] for b in range(spans)], weights[...])
-        mine = pl.ds(pl.multiple_of(24 + row, 8), TILE)
+        here = pl.ds(pl.multiple_of(24 + row, 8), TILE)
         for b, result in enumerate(results):
             for i in range(SPAN // 128):
                 piece = slice(i * 128, (i + 1) * 128)
-                ext[b * (SPAN // 128) + i, mine] = result[0:8, piece]
-                ext[lanes // 2 + b * (SPAN // 128) + i, mine] = result[8:16, piece]
+                ext[b * (SPAN // 128) + i, here] = result[0:8, piece]
+                ext[lanes // 2 + b * (SPAN // 128) + i, here] = result[8:16, piece]
+
+    for k in range(tiles):
+        exchange(k).wait_recv()
+        settle(k)
         halo(k, 0).start()
 
         @pl.when(has)
         def _():
             halo(k, 1).start()
 
-    for k in range(tiles):
-        halo(k, 0).wait_recv()
+    def settled(sems, side):
+        both = ext.at[:, 8 : 8 + half]
+        pltpu.make_async_copy(both, both, sems.at[side]).wait()
+
+    settled(halo_recv, 0)
 
     @pl.when(has)
     def _():
-        for k in range(tiles):
-            halo(k, 1).wait_recv()
-
-    for k in range(tiles):
-        exchange(k).wait_send()
-        halo(k, 0).wait_send()
+        settled(halo_recv, 1)
+
+    pltpu.make_async_copy(sent, sent, send_sem).wait()
+    settled(halo_send, 0)
 
     @pl.when(has)
     def _():
-        for k in range(tiles):
-            halo(k, 1).wait_send()
+        settled(halo_send, 1)
 
 
 def finish(
-    comp_red, comp_nir, chosen, ext, weights,
+    comp, ext, weights,
     out_red, out_nir, out_chosen, out_one, out_two, out_three,
-    level1, ext1, level2, ext2, one, two, three, sems,
+    level1, ext1, level2, ext2, one, two, three, comp_sem, sems,
 ):
-    pairs = ((comp_red, out_red), (comp_nir, out_nir), (chosen, out_chosen), (one, out_one), (two, out_two), (three, out_three))
+    for i, out in enumerate((out_red, out_nir, out_chosen)):
+        pltpu.make_async_copy(comp.at[i], out, comp_sem).start()
+    pairs = ((one, out_one), (two, out_two), (three, out_three))
     copies = [pltpu.make_async_copy(src, dst, sems.at[i]) for i, (src, dst) in enumerate(pairs)]
-    for copy in copies[:3]:
-        copy.start()
     core = lax.axis_index("dates")
     z = lax.axis_index("rows")
     has = jnp.where(core == 0, z > 0, z < lax.axis_size("rows") - 1)
@@ -277,17 +281,18 @@
                     ]
 
     descend(ext, 6, 24, 8, 8, one, level1, ext1)
-    copies[3].start()
+    copies[0].start()
     descend(ext1, 2, 8, 2, 2, two, level2, ext2)
-    copies[4].start()
+    copies[1].start()
     blocks = ext2.shape[0] // 2
     for band in range(2):
         for c in range(blocks):
             three[band, :, c * 128 : (c + 1) * 128] = stacked(ext2, band * blocks + c, 0, 2)
 
-    copies[5].start()
+    copies[2].start()
     for copy in copies:
         copy.wait()
+    pltpu.make_async_copy(comp, comp, comp_sem).wait()
 
 
 def body(red_band, nir_band, cloud_class, date_ordinal):
@@ -301,22 +306,26 @@
     arrays = [pltpu.with_memory_space_constraint(array, pltpu.HBM) for array in arrays]
     near = pl.pallas_call(
         kernel,
-        out_shape=[pltpu.VMEM((half, cols), i32)] * 3
-        + [pltpu.VMEM((cols // 128, 64, 128), f32), pltpu.VMEM((WINDOW, SPAN), jnp.bfloat16)],
+        out_shape=[
+            pltpu.VMEM((3, half, cols), i32),
+            pltpu.VMEM((cols // 128, 64, 128), f32),
+            pltpu.VMEM((WINDOW, SPAN), jnp.bfloat16),
+        ],
         in_specs=[far] * 4,
-        out_specs=[whole] * 5,
-        scratch_shapes=[pltpu.SMEM((dates,), i32)]
-        + [pltpu.VMEM((2 * tiles, dates, TILE, cols), i32)] * 3
-        + [
+        out_specs=[whole] * 3,
+        scratch_shapes=[
+            pltpu.SMEM((dates,), i32),
+            pltpu.VMEM((2 * tiles, 3, dates, TILE, cols), i32),
             pltpu.VMEM((tiles, 3, TILE, cols), i32),
             pltpu.VMEM((tiles, 3, TILE, cols), i32),
+            pltpu.VMEM((tiles, 6, TILE, cols), i32),
             pltpu.VMEM((16, cols + 256), f32),
-            pltpu.SemaphoreType.DMA((2 * tiles, cols // PART, 3)),
+            pltpu.SemaphoreType.DMA((cols // PART + 2 * tiles - 1,)),
+            pltpu.SemaphoreType.DMA,
             pltpu.SemaphoreType.DMA,
             pltpu.SemaphoreType.DMA((tiles,)),
-            pltpu.SemaphoreType.DMA((tiles,)),
-            pltpu.SemaphoreType.DMA((2, tiles)),
-            pltpu.SemaphoreType.DMA((2, tiles)),
+            pltpu.SemaphoreType.DMA((2,)),
+            pltpu.SemaphoreType.DMA((2,)),
         ],
         compiler_params=pltpu.CompilerParams(
             collective_id=0, has_side_effects=True, vmem_limit_bytes=32 * 1024 * 1024
@@ -327,7 +336,7 @@
     return pl.pallas_call(
         finish,
         out_shape=[jax.ShapeDtypeStruct((half, cols), i32)] * 3 + [jax.ShapeDtypeStruct(shape, f32) for shape in levels],
-        in_specs=[whole] * 5,
+        in_specs=[whole] * 3,
         out_specs=[far] * 6,
         scratch_shapes=[
             pltpu.VMEM((48, cols // 2 + 256), f32),
@@ -336,7 +345,7 @@
             pltpu.VMEM((cols // 512, 8, 128), f32),
         ]
         + [pltpu.VMEM(shape, f32) for shape in levels]
-        + [pltpu.SemaphoreType.DMA((6,))],
+        + [pltpu.SemaphoreType.DMA, pltpu.SemaphoreType.DMA((3,))],
         compiler_params=pltpu.CompilerParams(vmem_limit_bytes=16 * 1024 * 1024),
         name="finish",
     )(*near)

time: 29.4 us -> 28.8 us (0.980)
  Pallas kernels: 28.7 us -> 28 us
    pallas_call x1, Pallas kernels: 27.5 us -> 26.9 us  [body(): pl.pallas_call(kernel, out_shape=[pltpu.VMEM((3, half, cols), i32), pltpu...]
where the time goes in v4:
time: 28.8 us; the launch traced here: 28.7 us
  Pallas kernels  28 us (97%)
  between operations  0.64 us (2%)
    pallas_call x1, Pallas kernels, body(): pl.pallas_call(kernel, out_shape=[pltpu.VMEM((3, half, cols), i32), pltpu...  26.9 us
    pallas_call x1, Pallas kernels, body(): pl.pallas_call(finish, out_shape=[jax.ShapeDtypeStruct((half, cols), i32)...  1.13 us

profile of v4, /device:TPU:37, one launch (start us, length us, event | category | flops | bytes accessed | tf_op | source)
XLA Modules:
  0.0 28.7 jit_solution(8183734944522520370)
XLA Ops:
  0.6 26.9 %composite.1 = (s32[3,16,2048]{2,1,0:T(8,128)S(1)}, f32[16,64,128]{2,1,0:T(8,128)S(1)}, bf16[768,256]{1,0:T(8,128)(2,1)S(1)}) custom-call(s32[12]{0:T(128)} %ordinal_far.1, s32[12,32,2048]{2,1,0:T(8,128)} %red.1, s32[12,32,2048]{2,1,0:T(8,128)} %nir.1, s32[12,32,2048]{2,1,0:T(8,128)} %cloud.1), custom_call_target="tpu_custom_call" | custom-call | tf_op jit(solution)/shard_map/composite/pallas_call | solution.py:307
  27.5 1.1 %finish.1 = (s32[16,2048]{1,0:T(8,128)}, s32[16,2048]{1,0:T(8,128)}, s32[16,2048]{1,0:T(8,128)}, f32[2,8,1024]{2,1,0:T(8,128)}, f32[2,4,512]{2,1,0:T(4,128)}, /*index=5*/f32[2,2,256]{2,1,0:T(2,128)}) custom-call(s32[3,16,2048]{2,1,0:T(8,128)S(1)} %get-tuple-element.9.comp, f32[16,64,128]{2,1,0:T(8,128)S(1)} %get-tuple-element.10.ext, ...), custom_call_target="tpu_custom_call" | custom-call | tf_op jit(solution)/shard_map/finish/pallas_call | solution.py:336

commit v5 on v4

--- a/solution.py
+++ b/solution.py
@@ -16,7 +16,6 @@
 TAPS = (0.03125, 0.15625, 0.3125, 0.3125, 0.15625, 0.03125)
 TILE = 8
 GROUP = 512
-PART = 1024
 SPAN = 256
 WINDOW = 2 * SPAN + 256
 
@@ -29,13 +28,12 @@
     return (high << LIMB_BITS) | low
 
 
-def improve(best, new):
-    n1, n0, r1, r0, clear, order = best
-    m1, m0, s1, s0, fresh, index = new
+def improve(best, new, bar):
+    n1, n0, r1, r0, order = best
+    m1, m0, s1, s0, index = new
     low = m0 * r0 - n0 * s0 + ((order - index) >> 31)
     mid = (m1 * r0 + m0 * r1) - (n1 * s0 + n0 * s1) + (low >> LIMB_BITS)
-    top = m1 * r1 - n1 * s1 + (mid >> LIMB_BITS)
-    take = top >= clear - fresh
+    take = m1 * r1 - n1 * s1 + (mid >> LIMB_BITS) >= bar
     return tuple(jnp.where(take, one, two) for one, two in zip(new, best))
 
 
@@ -53,6 +51,12 @@
     rows = window[0].shape[0]
     out = jnp.dot(jnp.concatenate(parts, axis=0), weights, preferred_element_type=jnp.float32)
     return [out[2 * b * rows : (2 * b + 1) * rows] + out[(2 * b + 1) * rows : (2 * b + 2) * rows] for b in range(len(window))]
+
+
+def pieces_of(tiles, cols):
+    half = cols // 2
+    first = [(0, 0, GROUP), (0, GROUP, half - GROUP), (0, half, half), (1, 0, half), (1, half, half)]
+    return first + [(slot, 0, cols) for slot in range(2, 2 * tiles)]
 
 
 def kernel(
@@ -76,7 +80,7 @@
     def tile_in_half(c, k):
         return jnp.where(c == 0, k, tiles - 1 - k)
 
-    pieces = [(0, part, PART) for part in range(0, cols, PART)] + [(slot, 0, cols) for slot in range(1, 2 * tiles)]
+    pieces = pieces_of(tiles, cols)
 
     def load(i):
         slot, start, width = pieces[i]
@@ -109,7 +113,8 @@
     for i, weight in enumerate(TAPS):
         factor = jnp.where(tap == i, weight, factor)
     weights[...] = factor.astype(jnp.bfloat16)
-    clear_margins(level)
+    for k in range(tiles):
+        clear_margins(level.at[k])
     lanes = ext.shape[0]
     ext[:, 0:8] = jnp.zeros((lanes, 8, 128), jnp.float32)
     ext[:, 56:64] = jnp.zeros((lanes, 8, 128), jnp.float32)
@@ -119,11 +124,18 @@
         edge = pl.multiple_of(jnp.where(core == 0, 8, 40), 8)
         ext[:, pl.ds(edge, half)] = jnp.zeros((lanes, half, 128), jnp.float32)
 
-    def entry(slot, d, col):
-        m1, m0 = split(images[slot, 1, d, :, col])
-        s1, s0 = split(images[slot, 0, d, :, col])
-        fresh = jnp.where(images[slot, 2, d, :, col] == 0, CLEAR, 0)
-        return m1, m0, s1, s0, fresh, jnp.full((TILE, GROUP), ordinal[d], jnp.int32)
+    def best_of(slot, col):
+        lowest = images[slot, 2, 0, :, col]
+        for d in range(1, dates):
+            lowest = jnp.minimum(lowest, images[slot, 2, d, :, col])
+        limit = jnp.where(lowest == 0, 0, CLEAR)
+        best = None
+        for d in range(dates):
+            nir_value = jnp.where(images[slot, 2, d, :, col] > limit, 0, images[slot, 1, d, :, col])
+            order = jnp.full((TILE, GROUP), ordinal[d], jnp.int32)
+            new = (*split(nir_value), *split(images[slot, 0, d, :, col]), order)
+            best = new if best is None else improve(best, new, 0)
+        return best, lowest == 0
 
     def exchange(k):
         return pltpu.make_async_remote_copy(
@@ -138,17 +150,11 @@
     def columns(start, count):
         return [pl.ds(start + i * GROUP, GROUP) for i in range(count // GROUP)]
 
-    def best_of(slot, col):
-        best = entry(slot, 0, col)
-        for d in range(1, dates):
-            best = improve(best, entry(slot, d, col))
-        return best
-
     def offer(slot, col):
-        n1, n0, r1, r0, clear, order = best_of(slot, col)
+        (n1, n0, r1, r0, order), is_clear = best_of(slot, col)
         sent[slot, 0, :, col] = join(r1, r0)
         sent[slot, 1, :, col] = join(n1, n0)
-        sent[slot, 2, :, col] = order + jnp.where(clear > 0, FLAG_STEP, 0)
+        sent[slot, 2, :, col] = order + jnp.where(is_clear, FLAG_STEP, 0)
 
     order_copy.wait()
     for i, (slot, start, width) in enumerate(pieces):
@@ -165,7 +171,8 @@
     for k in range(tiles):
         loaded(base + k)
         for col in columns(0, cols):
-            for i, limb in enumerate(best_of(tiles + k, col)):
+            best, is_clear = best_of(tiles + k, col)
+            for i, limb in enumerate((*best, jnp.where(is_clear, CLEAR, 0))):
                 mine[k, i, :, col] = limb
 
     def halo(k, side):
@@ -185,24 +192,22 @@
         for col in columns(0, cols):
             flagged = got[k, 2, :, col]
             is_clear = flagged >= FLAG_STEP
-            theirs = (
-                *split(got[k, 1, :, col]),
-                *split(got[k, 0, :, col]),
-                jnp.where(is_clear, CLEAR, 0),
-                jnp.where(is_clear, flagged - FLAG_STEP, flagged),
-            )
-            n1, n0, r1, r0, _, order = improve(tuple(mine[k, i, :, col] for i in range(6)), theirs)
+            order = jnp.where(is_clear, flagged - FLAG_STEP, flagged)
+            theirs = (*split(got[k, 1, :, col]), *split(got[k, 0, :, col]), order)
+            bar = mine[k, 5, :, col] - jnp.where(is_clear, CLEAR, 0)
+            n1, n0, r1, r0, order = improve(tuple(mine[k, i, :, col] for i in range(5)), theirs, bar)
             value_red, value_nir = join(r1, r0), join(n1, n0)
             comp[0, pl.ds(row, TILE), col] = value_red
             comp[1, pl.ds(row, TILE), col] = value_nir
             comp[2, pl.ds(row, TILE), col] = order
             inner = pl.ds(col.start + 128, GROUP)
-            level[0:8, inner] = value_red.astype(jnp.float32) * SCALE_BAND
-            level[8:16, inner] = value_nir.astype(jnp.float32) * SCALE_BAND
-
+            level[k, 0:8, inner] = value_red.astype(jnp.float32) * SCALE_BAND
+            level[k, 8:16, inner] = value_nir.astype(jnp.float32) * SCALE_BAND
+
+    def narrow(k):
         spans = cols // 2 // SPAN
-        results = pooled([level[:, 2 * SPAN * b : 2 * SPAN * b + WINDOW] for b in range(spans)], weights[...])
-        here = pl.ds(pl.multiple_of(24 + row, 8), TILE)
+        results = pooled([level[k, :, 2 * SPAN * b : 2 * SPAN * b + WINDOW] for b in range(spans)], weights[...])
+        here = pl.ds(pl.multiple_of(24 + tile_in_half(core, k) * TILE, 8), TILE)
         for b, result in enumerate(results):
             for i in range(SPAN // 128):
                 piece = slice(i * 128, (i + 1) * 128)
@@ -211,12 +216,15 @@
 
     for k in range(tiles):
         exchange(k).wait_recv()
+    for k in range(tiles):
         settle(k)
-        halo(k, 0).start()
-
-        @pl.when(has)
+        narrow(k)
+    for side in range(2):
+
+        @pl.when((side == 0) | has)
         def _():
-            halo(k, 1).start()
+            for k in range(tiles):
+                halo(k, side).start()
 
     def settled(sems, side):
         both = ext.at[:, 8 : 8 + half]
@@ -319,8 +327,8 @@
             pltpu.VMEM((tiles, 3, TILE, cols), i32),
             pltpu.VMEM((tiles, 3, TILE, cols), i32),
             pltpu.VMEM((tiles, 6, TILE, cols), i32),
-            pltpu.VMEM((16, cols + 256), f32),
-            pltpu.SemaphoreType.DMA((cols // PART + 2 * tiles - 1,)),
+            pltpu.VMEM((tiles, 16, cols + 256), f32),
+            pltpu.SemaphoreType.DMA((len(pieces_of(tiles, cols)),)),
             pltpu.SemaphoreType.DMA,
             pltpu.SemaphoreType.DMA,
             pltpu.SemaphoreType.DMA((tiles,)),

time: 28.8 us -> 29 us (level)
  no operation moved by 1% of the time
where the time goes in v5:
time: 29 us; the launch traced here: 28.9 us
  Pallas kernels  28.2 us (97%)
  between operations  0.64 us (2%)
    pallas_call x1, Pallas kernels, body(): pl.pallas_call(kernel, out_shape=[pltpu.VMEM((3, half, cols), i32), pltpu...  27.1 us
    pallas_call x1, Pallas kernels, body(): pl.pallas_call(finish, out_shape=[jax.ShapeDtypeStruct((half, cols), i32)...  1.13 us

profile of v5, /device:TPU:37, one launch (start us, length us, event | category | flops | bytes accessed | tf_op | source)
XLA Modules:
  0.0 28.9 jit_solution(5761588049894310297)
XLA Ops:
  0.6 27.1 %composite.1 = (s32[3,16,2048]{2,1,0:T(8,128)S(1)}, f32[16,64,128]{2,1,0:T(8,128)S(1)}, bf16[768,256]{1,0:T(8,128)(2,1)S(1)}) custom-call(s32[12]{0:T(128)} %ordinal_far.1, s32[12,32,2048]{2,1,0:T(8,128)} %red.1, s32[12,32,2048]{2,1,0:T(8,128)} %nir.1, s32[12,32,2048]{2,1,0:T(8,128)} %cloud.1), custom_call_target="tpu_custom_call" | custom-call | tf_op jit(solution)/shard_map/composite/pallas_call | solution.py:315
  27.8 1.1 %finish.1 = (s32[16,2048]{1,0:T(8,128)}, s32[16,2048]{1,0:T(8,128)}, s32[16,2048]{1,0:T(8,128)}, f32[2,8,1024]{2,1,0:T(8,128)}, f32[2,4,512]{2,1,0:T(4,128)}, /*index=5*/f32[2,2,256]{2,1,0:T(2,128)}) custom-call(s32[3,16,2048]{2,1,0:T(8,128)S(1)} %get-tuple-element.9.comp, f32[16,64,128]{2,1,0:T(8,128)S(1)} %get-tuple-element.10.ext, ...), custom_call_target="tpu_custom_call" | custom-call | tf_op jit(solution)/shard_map/finish/pallas_call | solution.py:344

commit v6 on v5

--- a/solution.py
+++ b/solution.py
@@ -53,6 +53,44 @@
     return [out[2 * b * rows : (2 * b + 1) * rows] + out[(2 * b + 1) * rows : (2 * b + 2) * rows] for b in range(len(window))]
 
 
+def place():
+    core = lax.axis_index("dates")
+    z = lax.axis_index("rows")
+    return jnp.where(core == 0, z > 0, z < lax.axis_size("rows") - 1), core
+
+
+def inside(has, core, rows, near):
+    index = lax.broadcasted_iota(jnp.int32, (rows, 128), 0)
+    low = jnp.where(has | (core == 1), 0, near)
+    high = jnp.where(has | (core == 0), rows, rows - near)
+    return (index >= low) & (index < high)
+
+
+def stacked(source, block, start, rows):
+    value = TAPS[0] * source[block, pl.ds(start, rows, 2), :]
+    for i in range(1, 6):
+        value = value + TAPS[i] * source[block, pl.ds(start + i, rows, 2), :]
+    return value
+
+
+def descend(has, core, weights, source, start, rows, keep, near, out, padded, target):
+    valid = inside(has, core, rows, near)
+    blocks = source.shape[0] // 2
+    for band in range(2):
+        for c in range(blocks):
+            value = stacked(source, band * blocks + c, start, rows)
+            out[band, :, c * 128 : (c + 1) * 128] = value[keep : keep + out.shape[1]]
+            padded[band * rows : (band + 1) * rows, 128 * (c + 1) : 128 * (c + 2)] = jnp.where(valid, value, 0.0)
+    spans = blocks * 64 // SPAN
+    results = pooled([padded[:, 2 * SPAN * b : 2 * SPAN * b + WINDOW] for b in range(spans)], weights[...])
+    for b, result in enumerate(results):
+        for band in range(2):
+            for i in range(SPAN // 128):
+                target[band * blocks // 2 + b * (SPAN // 128) + i] = result[
+                    band * rows : (band + 1) * rows, i * 128 : (i + 1) * 128
+                ]
+
+
 def pieces_of(tiles, cols):
     half = cols // 2
     first = [(0, 0, GROUP), (0, GROUP, half - GROUP), (0, half, half), (1, 0, half), (1, half, half)]
@@ -61,8 +99,8 @@
 
 def kernel(
     ordinal_far, red, nir, cloud,
-    comp, ext, weights,
-    ordinal, images, sent, got, mine, level,
+    comp, one, ext1, weights,
+    ordinal, images, sent, got, mine, level, ext, level1,
     in_sem, ordinal_sem, send_sem, recv_sem, halo_send, halo_recv,
 ):
     dates, strip, cols = red.shape
@@ -113,8 +151,8 @@
     for i, weight in enumerate(TAPS):
         factor = jnp.where(tap == i, weight, factor)
     weights[...] = factor.astype(jnp.bfloat16)
-    for k in range(tiles):
-        clear_margins(level.at[k])
+    for buffer in (*(level.at[k] for k in range(tiles)), level1):
+        clear_margins(buffer)
     lanes = ext.shape[0]
     ext[:, 0:8] = jnp.zeros((lanes, 8, 128), jnp.float32)
     ext[:, 56:64] = jnp.zeros((lanes, 8, 128), jnp.float32)
@@ -137,10 +175,10 @@
             best = new if best is None else improve(best, new, 0)
         return best, lowest == 0
 
-    def exchange(k):
+    def exchange(k, col):
         return pltpu.make_async_remote_copy(
-            src_ref=sent.at[k],
-            dst_ref=got.at[k],
+            src_ref=sent.at[k, :, :, col],
+            dst_ref=got.at[k, :, :, col],
             send_sem=send_sem,
             recv_sem=recv_sem.at[k],
             device_id=partner,
@@ -162,10 +200,11 @@
             loaded(i)
             for col in columns(start, width):
                 offer(slot, col)
-            if start + width == cols:
-                if slot == 0:
-                    pl.semaphore_wait(barrier, jnp.where(has, 2, 1))
-                exchange(slot).start()
+            if slot == 0 and start + width == cols:
+                pl.semaphore_wait(barrier, jnp.where(has, 2, 1))
+                exchange(slot, pl.ds(0, cols)).start()
+            if slot > 0:
+                exchange(slot, pl.ds(start, width)).start()
 
     base = len(pieces) - tiles
     for k in range(tiles):
@@ -215,16 +254,14 @@
                 ext[lanes // 2 + b * (SPAN // 128) + i, here] = result[8:16, piece]
 
     for k in range(tiles):
-        exchange(k).wait_recv()
-    for k in range(tiles):
+        pltpu.make_async_copy(got.at[k], got.at[k], recv_sem.at[k]).wait()
         settle(k)
         narrow(k)
-    for side in range(2):
-
-        @pl.when((side == 0) | has)
+        halo(k, 0).start()
+
+        @pl.when(has)
         def _():
-            for k in range(tiles):
-                halo(k, side).start()
+            halo(k, 1).start()
 
     def settled(sems, side):
         both = ext.at[:, 8 : 8 + half]
@@ -236,6 +273,7 @@
     def _():
         settled(halo_recv, 1)
 
+    descend(has, core, weights, ext, 6, 24, 8, 8, one, level1, ext1)
     pltpu.make_async_copy(sent, sent, send_sem).wait()
     settled(halo_send, 0)
 
@@ -245,58 +283,23 @@
 
 
 def finish(
-    comp, ext, weights,
+    comp, one, ext1, weights,
     out_red, out_nir, out_chosen, out_one, out_two, out_three,
-    level1, ext1, level2, ext2, one, two, three, comp_sem, sems,
+    two, three, level2, ext2, comp_sem, sems,
 ):
+    pairs = ((one, out_one), (two, out_two), (three, out_three))
+    copies = [pltpu.make_async_copy(src, dst, sems.at[i]) for i, (src, dst) in enumerate(pairs)]
     for i, out in enumerate((out_red, out_nir, out_chosen)):
         pltpu.make_async_copy(comp.at[i], out, comp_sem).start()
-    pairs = ((one, out_one), (two, out_two), (three, out_three))
-    copies = [pltpu.make_async_copy(src, dst, sems.at[i]) for i, (src, dst) in enumerate(pairs)]
-    core = lax.axis_index("dates")
-    z = lax.axis_index("rows")
-    has = jnp.where(core == 0, z > 0, z < lax.axis_size("rows") - 1)
-    clear_margins(level1)
+    copies[0].start()
+    has, core = place()
     clear_margins(level2)
-
-    def inside(rows, near):
-        index = lax.broadcasted_iota(jnp.int32, (rows, 128), 0)
-        low = jnp.where(has | (core == 1), 0, near)
-        high = jnp.where(has | (core == 0), rows, rows - near)
-        return (index >= low) & (index < high)
-
-    def stacked(source, block, start, rows):
-        value = TAPS[0] * source[block, pl.ds(start, rows, 2), :]
-        for i in range(1, 6):
-            value = value + TAPS[i] * source[block, pl.ds(start + i, rows, 2), :]
-        return value
-
-    def descend(source, start, rows, keep, near, out, padded, target):
-        valid = inside(rows, near)
-        blocks = source.shape[0] // 2
-        for band in range(2):
-            for c in range(blocks):
-                value = stacked(source, band * blocks + c, start, rows)
-                out[band, :, c * 128 : (c + 1) * 128] = value[keep : keep + out.shape[1]]
-                padded[band * rows : (band + 1) * rows, 128 * (c + 1) : 128 * (c + 2)] = jnp.where(valid, value, 0.0)
-        spans = blocks * 64 // SPAN
-        results = pooled([padded[:, 2 * SPAN * b : 2 * SPAN * b + WINDOW] for b in range(spans)], weights[...])
-        for b, result in enumerate(results):
-            for band in range(2):
-                for i in range(SPAN // 128):
-                    target[band * blocks // 2 + b * (SPAN // 128) + i] = result[
-                        band * rows : (band + 1) * rows, i * 128 : (i + 1) * 128
-                    ]
-
-    descend(ext, 6, 24, 8, 8, one, level1, ext1)
-    copies[0].start()
-    descend(ext1, 2, 8, 2, 2, two, level2, ext2)
+    descend(has, core, weights, ext1, 2, 8, 2, 2, two, level2, ext2)
     copies[1].start()
     blocks = ext2.shape[0] // 2
     for band in range(2):
         for c in range(blocks):
             three[band, :, c * 128 : (c + 1) * 128] = stacked(ext2, band * blocks + c, 0, 2)
-
     copies[2].start()
     for copy in copies:
         copy.wait()
@@ -312,15 +315,17 @@
     f32, i32 = jnp.float32, jnp.int32
     arrays = (date_ordinal, red_band, nir_band, cloud_class)
     arrays = [pltpu.with_memory_space_constraint(array, pltpu.HBM) for array in arrays]
+    levels = [(2, half >> k, cols >> k) for k in (1, 2, 3)]
     near = pl.pallas_call(
         kernel,
         out_shape=[
             pltpu.VMEM((3, half, cols), i32),
-            pltpu.VMEM((cols // 128, 64, 128), f32),
+            pltpu.VMEM(levels[0], f32),
+            pltpu.VMEM((cols // 256, 24, 128), f32),
             pltpu.VMEM((WINDOW, SPAN), jnp.bfloat16),
         ],
         in_specs=[far] * 4,
-        out_specs=[whole] * 3,
+        out_specs=[whole] * 4,
         scratch_shapes=[
             pltpu.SMEM((dates,), i32),
             pltpu.VMEM((2 * tiles, 3, dates, TILE, cols), i32),
@@ -328,6 +333,8 @@
             pltpu.VMEM((tiles, 3, TILE, cols), i32),
             pltpu.VMEM((tiles, 6, TILE, cols), i32),
             pltpu.VMEM((tiles, 16, cols + 256), f32),
+            pltpu.VMEM((cols // 128, 64, 128), f32),
+            pltpu.VMEM((48, cols // 2 + 256), f32),
             pltpu.SemaphoreType.DMA((len(pieces_of(tiles, cols)),)),
             pltpu.SemaphoreType.DMA,
             pltpu.SemaphoreType.DMA,
@@ -340,20 +347,19 @@
         ),
         name="composite",
     )(*arrays)
-    levels = [(2, half >> k, cols >> k) for k in (1, 2, 3)]
     return pl.pallas_call(
         finish,
         out_shape=[jax.ShapeDtypeStruct((half, cols), i32)] * 3 + [jax.ShapeDtypeStruct(shape, f32) for shape in levels],
-        in_specs=[whole] * 3,
+        in_specs=[whole] * 4,
         out_specs=[far] * 6,
         scratch_shapes=[
-            pltpu.VMEM((48, cols // 2 + 256), f32),
-            pltpu.VMEM((cols // 256, 24, 128), f32),
+            pltpu.VMEM(levels[1], f32),
+            pltpu.VMEM(levels[2], f32),
             pltpu.VMEM((16, cols // 4 + 256), f32),
             pltpu.VMEM((cols // 512, 8, 128), f32),
-        ]
-        + [pltpu.VMEM(shape, f32) for shape in levels]
-        + [pltpu.SemaphoreType.DMA, pltpu.SemaphoreType.DMA((3,))],
+            pltpu.SemaphoreType.DMA,
+            pltpu.SemaphoreType.DMA((3,)),
+        ],
         compiler_params=pltpu.CompilerParams(vmem_limit_bytes=16 * 1024 * 1024),
         name="finish",
     )(*near)

time: 29 us -> 28.8 us (level)
  no operation moved by 1% of the time
where the time goes in v6:
time: 28.8 us; the launch traced here: 28.7 us
  Pallas kernels  28 us (97%)
  between operations  0.64 us (2%)
    pallas_call x1, Pallas kernels, body(): pl.pallas_call(kernel, out_shape=[pltpu.VMEM((3, half, cols), i32), pltpu...  27.2 us
    pallas_call x1, Pallas kernels, body(): pl.pallas_call(finish, out_shape=[jax.ShapeDtypeStruct((half, cols), i32)...  0.84 us

profile of v6, /device:TPU:37, one launch (start us, length us, event | category | flops | bytes accessed | tf_op | source)
XLA Modules:
  0.0 28.7 jit_solution(13761214642767818135)
XLA Ops:
  0.6 27.2 %composite.1 = (s32[3,16,2048]{2,1,0:T(8,128)S(1)}, f32[2,8,1024]{2,1,0:T(8,128)S(1)}, f32[8,24,128]{2,1,0:T(8,128)S(1)}, bf16[768,256]{1,0:T(8,128)(2,1)S(1)}) custom-call(s32[12]{0:T(128)} %ordinal_far.1, s32[12,32,2048]{2,1,0:T(8,128)} %red.1, s32[12,32,2048]{2,1,0:T(8,128)} %nir.1, s32[12,32,2048]{2,1,0:T(8,128)} %cloud.1), custom_call_target="tpu_custom_call" | custom-call | tf_op jit(solution)/shard_map/composite/pallas_call | solution.py:319
  27.8 0.8 %finish.1 = (s32[16,2048]{1,0:T(8,128)}, s32[16,2048]{1,0:T(8,128)}, s32[16,2048]{1,0:T(8,128)}, f32[2,8,1024]{2,1,0:T(8,128)}, f32[2,4,512]{2,1,0:T(4,128)}, /*index=5*/f32[2,2,256]{2,1,0:T(2,128)}) custom-call(s32[3,16,2048]{2,1,0:T(8,128)S(1)} %get-tuple-element.10.comp, f32[2,8,1024]{2,1,0:T(8,128)S(1)} %get-tuple-element.11.one, ...), custom_call_target="tpu_custom_call" | custom-call | tf_op jit(solution)/shard_map/finish/pallas_call | solution.py:350

commit v7 on v6

--- a/solution.py
+++ b/solution.py
@@ -12,10 +12,11 @@
 LIMB_MASK = 32767
 CLEAR = 1 << 30
 FLAG_STEP = 32
+RADIX_BITS = 4
 SCALE_BAND = 9.313225746154785e-10
 TAPS = (0.03125, 0.15625, 0.3125, 0.3125, 0.15625, 0.03125)
 TILE = 8
-GROUP = 512
+GROUP = 256
 SPAN = 256
 WINDOW = 2 * SPAN + 256
 
@@ -26,6 +27,15 @@
 
 def join(high, low):
     return (high << LIMB_BITS) | low
+
+
+def younger(best, new):
+    n1, n0, r1, r0, _ = best
+    m1, m0, s1, s0, _ = new
+    low = n0 * s0 - m0 * r0
+    mid = (n1 * s0 + n0 * s1) - (m1 * r0 + m0 * r1) + (low >> LIMB_BITS)
+    take = n1 * s1 - m1 * r1 + (mid >> LIMB_BITS) < 0
+    return tuple(jnp.where(take, one, two) for one, two in zip(new, best))
 
 
 def improve(best, new, bar):
@@ -91,17 +101,30 @@
                 ]
 
 
+def network(count):
+    pairs, p = [], 1
+    while p < count:
+        k = p
+        while k >= 1:
+            for j in range(k % p, count - k, 2 * k):
+                for i in range(j, j + min(k, count - j - k)):
+                    if i // (2 * p) == (i + k) // (2 * p):
+                        pairs.append((i, i + k))
+            k //= 2
+        p *= 2
+    return pairs
+
+
 def pieces_of(tiles, cols):
-    half = cols // 2
-    first = [(0, 0, GROUP), (0, GROUP, half - GROUP), (0, half, half), (1, 0, half), (1, half, half)]
-    return first + [(slot, 0, cols) for slot in range(2, 2 * tiles)]
+    widths = [4 * GROUP, 4 * GROUP, 4 * GROUP] + [cols] * (2 * tiles - 3)
+    return [(slot, col, width) for slot, width in enumerate(widths) for col in range(0, cols, width)]
 
 
 def kernel(
     ordinal_far, red, nir, cloud,
     comp, one, ext1, weights,
-    ordinal, images, sent, got, mine, level, ext, level1,
-    in_sem, ordinal_sem, send_sem, recv_sem, halo_send, halo_recv,
+    ordinal, ranked, sent, got, mine, level, ext, level1,
+    in_sem, ordinal_sem, send_sem, recv_sem, halo_send, halo_recv, *images
 ):
     dates, strip, cols = red.shape
     half = strip // 2
@@ -126,12 +149,10 @@
         row = pl.multiple_of(owner * half + tile_in_half(owner, slot % tiles) * TILE, TILE)
         col = pl.ds(start, width)
         for j, src in enumerate((red, nir, cloud)):
-            pltpu.make_async_copy(src.at[:, pl.ds(row, TILE), col], images.at[slot, j, :, :, col], in_sem.at[i]).start()
+            pltpu.make_async_copy(src.at[:, pl.ds(row, TILE), col], images[i].at[j], in_sem.at[i]).start()
 
     def loaded(i):
-        slot, start, width = pieces[i]
-        there = images.at[slot, :, :, :, pl.ds(start, width)]
-        pltpu.make_async_copy(there, there, in_sem.at[i]).wait()
+        pltpu.make_async_copy(images[i], images[i], in_sem.at[i]).wait()
 
     order_copy = pltpu.make_async_copy(ordinal_far, ordinal, ordinal_sem)
     order_copy.start()
@@ -162,18 +183,19 @@
         edge = pl.multiple_of(jnp.where(core == 0, 8, 40), 8)
         ext[:, pl.ds(edge, half)] = jnp.zeros((lanes, half, 128), jnp.float32)
 
-    def best_of(slot, col):
-        lowest = images[slot, 2, 0, :, col]
+    def best_of(image, col):
+        product = image[2, 0, :, col]
         for d in range(1, dates):
-            lowest = jnp.minimum(lowest, images[slot, 2, d, :, col])
-        limit = jnp.where(lowest == 0, 0, CLEAR)
+            product = product * image[2, d, :, col]
+        limit = jnp.where(product == 0, 0, CLEAR)
         best = None
         for d in range(dates):
-            nir_value = jnp.where(images[slot, 2, d, :, col] > limit, 0, images[slot, 1, d, :, col])
-            order = jnp.full((TILE, GROUP), ordinal[d], jnp.int32)
-            new = (*split(nir_value), *split(images[slot, 0, d, :, col]), order)
-            best = new if best is None else improve(best, new, 0)
-        return best, lowest == 0
+            at = ranked[0, d]
+            nir_value = jnp.where(image[2, at, :, col] > limit, 0, image[1, at, :, col])
+            order = jnp.full((TILE, GROUP), ranked[1, d], jnp.int32)
+            new = (*split(nir_value), *split(image[0, at, :, col]), order)
+            best = new if best is None else younger(best, new)
+        return best, product == 0
 
     def exchange(k, col):
         return pltpu.make_async_remote_copy(
@@ -188,31 +210,37 @@
     def columns(start, count):
         return [pl.ds(start + i * GROUP, GROUP) for i in range(count // GROUP)]
 
-    def offer(slot, col):
-        (n1, n0, r1, r0, order), is_clear = best_of(slot, col)
+    def offer(i, slot, col, inner):
+        (n1, n0, r1, r0, order), is_clear = best_of(images[i], inner)
         sent[slot, 0, :, col] = join(r1, r0)
         sent[slot, 1, :, col] = join(n1, n0)
         sent[slot, 2, :, col] = order + jnp.where(is_clear, FLAG_STEP, 0)
 
     order_copy.wait()
+    keys = [(ordinal[d] << RADIX_BITS) + d for d in range(dates)]
+    for i, j in network(dates):
+        keys[i], keys[j] = jnp.minimum(keys[i], keys[j]), jnp.maximum(keys[i], keys[j])
+    for d, key in enumerate(keys):
+        ranked[0, d] = key & ((1 << RADIX_BITS) - 1)
+        ranked[1, d] = key >> RADIX_BITS
     for i, (slot, start, width) in enumerate(pieces):
         if slot < tiles:
             loaded(i)
-            for col in columns(start, width):
-                offer(slot, col)
+            for col, inner in zip(columns(start, width), columns(0, width)):
+                offer(i, slot, col, inner)
             if slot == 0 and start + width == cols:
                 pl.semaphore_wait(barrier, jnp.where(has, 2, 1))
                 exchange(slot, pl.ds(0, cols)).start()
             if slot > 0:
                 exchange(slot, pl.ds(start, width)).start()
 
-    base = len(pieces) - tiles
-    for k in range(tiles):
-        loaded(base + k)
-        for col in columns(0, cols):
-            best, is_clear = best_of(tiles + k, col)
-            for i, limb in enumerate((*best, jnp.where(is_clear, CLEAR, 0))):
-                mine[k, i, :, col] = limb
+    for i, (slot, start, width) in enumerate(pieces):
+        if slot >= tiles:
+            loaded(i)
+            for col, inner in zip(columns(start, width), columns(0, width)):
+                best, is_clear = best_of(images[i], inner)
+                for j, limb in enumerate((*best, jnp.where(is_clear, CLEAR, 0))):
+                    mine[slot - tiles, j, :, col] = limb
 
     def halo(k, side):
         here = tile_in_half(core, k) * TILE
@@ -328,7 +356,7 @@
         out_specs=[whole] * 4,
         scratch_shapes=[
             pltpu.SMEM((dates,), i32),
-            pltpu.VMEM((2 * tiles, 3, dates, TILE, cols), i32),
+            pltpu.SMEM((2, dates), i32),
             pltpu.VMEM((tiles, 3, TILE, cols), i32),
             pltpu.VMEM((tiles, 3, TILE, cols), i32),
             pltpu.VMEM((tiles, 6, TILE, cols), i32),
@@ -341,7 +369,8 @@
             pltpu.SemaphoreType.DMA((tiles,)),
             pltpu.SemaphoreType.DMA((2,)),
             pltpu.SemaphoreType.DMA((2,)),
-        ],
+        ]
+        + [pltpu.VMEM((3, dates, TILE, width), i32) for _, _, width in pieces_of(tiles, cols)],
         compiler_params=pltpu.CompilerParams(
             collective_id=0, has_side_effects=True, vmem_limit_bytes=32 * 1024 * 1024
         ),

time: 28.8 us -> 28.4 us (0.986)
  Pallas kernels: 28 us -> 27.7 us
    pallas_call x1, Pallas kernels: 27.2 us -> 26.9 us  [body(): pl.pallas_call(kernel, out_shape=[pltpu.VMEM((3, half, cols), i32), pltpu...]
where the time goes in v7:
time: 28.4 us; the launch traced here: 28.3 us
  Pallas kernels  27.7 us (98%)
  between operations  0.64 us (2%)
    pallas_call x1, Pallas kernels, body(): pl.pallas_call(kernel, out_shape=[pltpu.VMEM((3, half, cols), i32), pltpu...  26.9 us
    pallas_call x1, Pallas kernels, body(): pl.pallas_call(finish, out_shape=[jax.ShapeDtypeStruct((half, cols), i32)...  0.84 us

profile of v7, /device:TPU:37, one launch (start us, length us, event | category | flops | bytes accessed | tf_op | source)
XLA Modules:
  0.0 28.3 jit_solution(11627850765730228500)
XLA Ops:
  0.6 26.9 %composite.1 = (s32[3,16,2048]{2,1,0:T(8,128)S(1)}, f32[2,8,1024]{2,1,0:T(8,128)S(1)}, f32[8,24,128]{2,1,0:T(8,128)S(1)}, bf16[768,256]{1,0:T(8,128)(2,1)S(1)}) custom-call(s32[12]{0:T(128)} %ordinal_far.1, s32[12,32,2048]{2,1,0:T(8,128)} %red.1, s32[12,32,2048]{2,1,0:T(8,128)} %nir.1, s32[12,32,2048]{2,1,0:T(8,128)} %cloud.1), custom_call_target="tpu_custom_call" | custom-call | tf_op jit(solution)/shard_map/composite/pallas_call | solution.py:347
  27.5 0.8 %finish.1 = (s32[16,2048]{1,0:T(8,128)}, s32[16,2048]{1,0:T(8,128)}, s32[16,2048]{1,0:T(8,128)}, f32[2,8,1024]{2,1,0:T(8,128)}, f32[2,4,512]{2,1,0:T(4,128)}, /*index=5*/f32[2,2,256]{2,1,0:T(2,128)}) custom-call(s32[3,16,2048]{2,1,0:T(8,128)S(1)} %get-tuple-element.10.comp, f32[2,8,1024]{2,1,0:T(8,128)S(1)} %get-tuple-element.11.one, ...), custom_call_target="tpu_custom_call" | custom-call | tf_op jit(solution)/shard_map/finish/pallas_call | solution.py:379

commit v8 on v7

--- a/solution.py
+++ b/solution.py
@@ -96,7 +96,7 @@
     for b, result in enumerate(results):
         for band in range(2):
             for i in range(SPAN // 128):
-                target[band * blocks // 2 + b * (SPAN // 128) + i] = result[
+                target[band * blocks // 2 + b * (SPAN // 128) + i, 0:rows] = result[
                     band * rows : (band + 1) * rows, i * 128 : (i + 1) * 128
                 ]
 
@@ -172,7 +172,7 @@
     for i, weight in enumerate(TAPS):
         factor = jnp.where(tap == i, weight, factor)
     weights[...] = factor.astype(jnp.bfloat16)
-    for buffer in (*(level.at[k] for k in range(tiles)), level1):
+    for buffer in (*(level.at[k] for k in range(tiles + 1)), level1):
         clear_margins(buffer)
     lanes = ext.shape[0]
     ext[:, 0:8] = jnp.zeros((lanes, 8, 128), jnp.float32)
@@ -210,11 +210,11 @@
     def columns(start, count):
         return [pl.ds(start + i * GROUP, GROUP) for i in range(count // GROUP)]
 
-    def offer(i, slot, col, inner):
-        (n1, n0, r1, r0, order), is_clear = best_of(images[i], inner)
-        sent[slot, 0, :, col] = join(r1, r0)
-        sent[slot, 1, :, col] = join(n1, n0)
-        sent[slot, 2, :, col] = order + jnp.where(is_clear, FLAG_STEP, 0)
+    def offer(best, is_clear, k, col):
+        n1, n0, r1, r0, order = best
+        sent[k, 0, :, col] = join(r1, r0)
+        sent[k, 1, :, col] = join(n1, n0)
+        sent[k, 2, :, col] = order + jnp.where(is_clear, FLAG_STEP, 0)
 
     order_copy.wait()
     keys = [(ordinal[d] << RADIX_BITS) + d for d in range(dates)]
@@ -227,7 +227,7 @@
         if slot < tiles:
             loaded(i)
             for col, inner in zip(columns(start, width), columns(0, width)):
-                offer(i, slot, col, inner)
+                offer(*best_of(images[i], inner), slot, col)
             if slot == 0 and start + width == cols:
                 pl.semaphore_wait(barrier, jnp.where(has, 2, 1))
                 exchange(slot, pl.ds(0, cols)).start()
@@ -241,6 +241,9 @@
                 best, is_clear = best_of(images[i], inner)
                 for j, limb in enumerate((*best, jnp.where(is_clear, CLEAR, 0))):
                     mine[slot - tiles, j, :, col] = limb
+                if slot == 2 * tiles - 1:
+                    offer(best, is_clear, tiles, col)
+    exchange(tiles, pl.ds(0, cols)).start()
 
     def halo(k, side):
         here = tile_in_half(core, k) * TILE
@@ -254,27 +257,40 @@
             device_id_type=MESH,
         )
 
+    def unpack(packed, k, col):
+        flagged = packed[k, 2, :, col]
+        is_clear = flagged >= FLAG_STEP
+        order = jnp.where(is_clear, flagged - FLAG_STEP, flagged)
+        return (*split(packed[k, 1, :, col]), *split(packed[k, 0, :, col]), order), jnp.where(is_clear, CLEAR, 0)
+
+    def fill(k, col, value_red, value_nir):
+        inner = pl.ds(col.start + 128, GROUP)
+        level[k, 0:8, inner] = value_red.astype(jnp.float32) * SCALE_BAND
+        level[k, 8:16, inner] = value_nir.astype(jnp.float32) * SCALE_BAND
+
     def settle(k):
         row = pl.multiple_of(tile_in_half(core, k) * TILE, TILE)
         for col in columns(0, cols):
-            flagged = got[k, 2, :, col]
-            is_clear = flagged >= FLAG_STEP
-            order = jnp.where(is_clear, flagged - FLAG_STEP, flagged)
-            theirs = (*split(got[k, 1, :, col]), *split(got[k, 0, :, col]), order)
-            bar = mine[k, 5, :, col] - jnp.where(is_clear, CLEAR, 0)
+            theirs, fresh = unpack(got, k, col)
+            bar = mine[k, 5, :, col] - fresh
             n1, n0, r1, r0, order = improve(tuple(mine[k, i, :, col] for i in range(5)), theirs, bar)
             value_red, value_nir = join(r1, r0), join(n1, n0)
             comp[0, pl.ds(row, TILE), col] = value_red
             comp[1, pl.ds(row, TILE), col] = value_nir
             comp[2, pl.ds(row, TILE), col] = order
-            inner = pl.ds(col.start + 128, GROUP)
-            level[k, 0:8, inner] = value_red.astype(jnp.float32) * SCALE_BAND
-            level[k, 8:16, inner] = value_nir.astype(jnp.float32) * SCALE_BAND
-
-    def narrow(k):
+            fill(k, col, value_red, value_nir)
+
+    def settle_beside():
+        for col in columns(0, cols):
+            ours, clear = unpack(sent, tiles - 1, col)
+            theirs, fresh = unpack(got, tiles, col)
+            n1, n0, r1, r0, _ = improve(ours, theirs, clear - fresh)
+            fill(tiles, col, join(r1, r0), join(n1, n0))
+
+    def narrow(k, row):
         spans = cols // 2 // SPAN
         results = pooled([level[k, :, 2 * SPAN * b : 2 * SPAN * b + WINDOW] for b in range(spans)], weights[...])
-        here = pl.ds(pl.multiple_of(24 + tile_in_half(core, k) * TILE, 8), TILE)
+        here = pl.ds(pl.multiple_of(row, 8), TILE)
         for b, result in enumerate(results):
             for i in range(SPAN // 128):
                 piece = slice(i * 128, (i + 1) * 128)
@@ -284,16 +300,21 @@
     for k in range(tiles):
         pltpu.make_async_copy(got.at[k], got.at[k], recv_sem.at[k]).wait()
         settle(k)
-        narrow(k)
-        halo(k, 0).start()
+        narrow(k, 24 + tile_in_half(core, k) * TILE)
+        if k < tiles - 1:
+            halo(k, 0).start()
 
         @pl.when(has)
         def _():
             halo(k, 1).start()
 
+    pltpu.make_async_copy(got.at[tiles], got.at[tiles], recv_sem.at[tiles]).wait()
+    settle_beside()
+    narrow(tiles, 8 + 32 * other + tile_in_half(other, tiles - 1) * TILE)
+
     def settled(sems, side):
-        both = ext.at[:, 8 : 8 + half]
-        pltpu.make_async_copy(both, both, sems.at[side]).wait()
+        rows = ext.at[:, 8 : 8 + (half if side == 1 else half - TILE)]
+        pltpu.make_async_copy(rows, rows, sems.at[side]).wait()
 
     settled(halo_recv, 0)
 
@@ -357,16 +378,16 @@
         scratch_shapes=[
             pltpu.SMEM((dates,), i32),
             pltpu.SMEM((2, dates), i32),
-            pltpu.VMEM((tiles, 3, TILE, cols), i32),
-            pltpu.VMEM((tiles, 3, TILE, cols), i32),
+            pltpu.VMEM((tiles + 1, 3, TILE, cols), i32),
+            pltpu.VMEM((tiles + 1, 3, TILE, cols), i32),
             pltpu.VMEM((tiles, 6, TILE, cols), i32),
-            pltpu.VMEM((tiles, 16, cols + 256), f32),
+            pltpu.VMEM((tiles + 1, 16, cols + 256), f32),
             pltpu.VMEM((cols // 128, 64, 128), f32),
             pltpu.VMEM((48, cols // 2 + 256), f32),
             pltpu.SemaphoreType.DMA((len(pieces_of(tiles, cols)),)),
             pltpu.SemaphoreType.DMA,
             pltpu.SemaphoreType.DMA,
-            pltpu.SemaphoreType.DMA((tiles,)),
+            pltpu.SemaphoreType.DMA((tiles + 1,)),
             pltpu.SemaphoreType.DMA((2,)),
             pltpu.SemaphoreType.DMA((2,)),
         ]
@@ -385,7 +406,7 @@
             pltpu.VMEM(levels[1], f32),
             pltpu.VMEM(levels[2], f32),
             pltpu.VMEM((16, cols // 4 + 256), f32),
-            pltpu.VMEM((cols // 512, 8, 128), f32),
+            pltpu.VMEM((cols // 512, 24, 128), f32),
             pltpu.SemaphoreType.DMA,
             pltpu.SemaphoreType.DMA((3,)),
         ],

time: 28.4 us -> 28.4 us (level)
  no operation moved by 1% of the time
where the time goes in v8:
time: 28.4 us; the launch traced here: 28.3 us
  Pallas kernels  27.6 us (97%)
  between operations  0.64 us (2%)
    pallas_call x1, Pallas kernels, body(): pl.pallas_call(kernel, out_shape=[pltpu.VMEM((3, half, cols), i32), pltpu...  26.8 us
    pallas_call x1, Pallas kernels, body(): pl.pallas_call(finish, out_shape=[jax.ShapeDtypeStruct((half, cols), i32)...  0.84 us

profile of v8, /device:TPU:37, one launch (start us, length us, event | category | flops | bytes accessed | tf_op | source)
XLA Modules:
  0.0 28.3 jit_solution(4837728187326581740)
XLA Ops:
  0.6 26.8 %composite.1 = (s32[3,16,2048]{2,1,0:T(8,128)S(1)}, f32[2,8,1024]{2,1,0:T(8,128)S(1)}, f32[8,24,128]{2,1,0:T(8,128)S(1)}, bf16[768,256]{1,0:T(8,128)(2,1)S(1)}) custom-call(s32[12]{0:T(128)} %ordinal_far.1, s32[12,32,2048]{2,1,0:T(8,128)} %red.1, s32[12,32,2048]{2,1,0:T(8,128)} %nir.1, s32[12,32,2048]{2,1,0:T(8,128)} %cloud.1), custom_call_target="tpu_custom_call" | custom-call | tf_op jit(solution)/shard_map/composite/pallas_call | solution.py:368
  27.4 0.8 %finish.1 = (s32[16,2048]{1,0:T(8,128)}, s32[16,2048]{1,0:T(8,128)}, s32[16,2048]{1,0:T(8,128)}, f32[2,8,1024]{2,1,0:T(8,128)}, f32[2,4,512]{2,1,0:T(4,128)}, /*index=5*/f32[2,2,256]{2,1,0:T(2,128)}) custom-call(s32[3,16,2048]{2,1,0:T(8,128)S(1)} %get-tuple-element.10.comp, f32[2,8,1024]{2,1,0:T(8,128)S(1)} %get-tuple-element.11.one, ...), custom_call_target="tpu_custom_call" | custom-call | tf_op jit(solution)/shard_map/finish/pallas_call | solution.py:400

commit v9 on v8

--- a/solution.py
+++ b/solution.py
@@ -16,6 +16,7 @@
 SCALE_BAND = 9.313225746154785e-10
 TAPS = (0.03125, 0.15625, 0.3125, 0.3125, 0.15625, 0.03125)
 TILE = 8
+REACH = 6
 GROUP = 256
 SPAN = 256
 WINDOW = 2 * SPAN + 256
@@ -257,6 +258,18 @@
             device_id_type=MESH,
         )
 
+    def far_halo(c):
+        here = (tiles - 1) * TILE if c == 0 else TILE - REACH
+        there = 8 + 32 * (1 - c) + here
+        return pltpu.make_async_remote_copy(
+            src_ref=ext.at[:, 24 + here : 24 + here + REACH],
+            dst_ref=ext.at[:, there : there + REACH],
+            send_sem=halo_send.at[1],
+            recv_sem=halo_recv.at[1],
+            device_id=neighbour,
+            device_id_type=MESH,
+        )
+
     def unpack(packed, k, col):
         flagged = packed[k, 2, :, col]
         is_clear = flagged >= FLAG_STEP
@@ -304,16 +317,18 @@
         if k < tiles - 1:
             halo(k, 0).start()
 
-        @pl.when(has)
-        def _():
-            halo(k, 1).start()
+        for c in range(2):
+
+            @pl.when(has & (core == c))
+            def _():
+                (halo(k, 1) if k < tiles - 1 else far_halo(c)).start()
 
     pltpu.make_async_copy(got.at[tiles], got.at[tiles], recv_sem.at[tiles]).wait()
     settle_beside()
     narrow(tiles, 8 + 32 * other + tile_in_half(other, tiles - 1) * TILE)
 
     def settled(sems, side):
-        rows = ext.at[:, 8 : 8 + (half if side == 1 else half - TILE)]
+        rows = ext.at[:, 8 : 8 + half - TILE + (REACH if side == 1 else 0)]
         pltpu.make_async_copy(rows, rows, sems.at[side]).wait()
 
     settled(halo_recv, 0)

time: 28.4 us -> 28.4 us (level)
  no operation moved by 1% of the time
where the time goes in v9:
time: 28.4 us; the launch traced here: 28.3 us
  Pallas kernels  27.6 us (97%)
  between operations  0.64 us (2%)
    pallas_call x1, Pallas kernels, body(): pl.pallas_call(kernel, out_shape=[pltpu.VMEM((3, half, cols), i32), pltpu...  26.8 us
    pallas_call x1, Pallas kernels, body(): pl.pallas_call(finish, out_shape=[jax.ShapeDtypeStruct((half, cols), i32)...  0.84 us

profile of v9, /device:TPU:37, one launch (start us, length us, event | category | flops | bytes accessed | tf_op | source)
XLA Modules:
  0.0 28.3 jit_solution(14110853885340894588)
XLA Ops:
  0.6 26.8 %composite.1 = (s32[3,16,2048]{2,1,0:T(8,128)S(1)}, f32[2,8,1024]{2,1,0:T(8,128)S(1)}, f32[8,24,128]{2,1,0:T(8,128)S(1)}, bf16[768,256]{1,0:T(8,128)(2,1)S(1)}) custom-call(s32[12]{0:T(128)} %ordinal_far.1, s32[12,32,2048]{2,1,0:T(8,128)} %red.1, s32[12,32,2048]{2,1,0:T(8,128)} %nir.1, s32[12,32,2048]{2,1,0:T(8,128)} %cloud.1), custom_call_target="tpu_custom_call" | custom-call | tf_op jit(solution)/shard_map/composite/pallas_call | solution.py:383
  27.4 0.8 %finish.1 = (s32[16,2048]{1,0:T(8,128)}, s32[16,2048]{1,0:T(8,128)}, s32[16,2048]{1,0:T(8,128)}, f32[2,8,1024]{2,1,0:T(8,128)}, f32[2,4,512]{2,1,0:T(4,128)}, /*index=5*/f32[2,2,256]{2,1,0:T(2,128)}) custom-call(s32[3,16,2048]{2,1,0:T(8,128)S(1)} %get-tuple-element.10.comp, f32[2,8,1024]{2,1,0:T(8,128)S(1)} %get-tuple-element.11.one, ...), custom_call_target="tpu_custom_call" | custom-call | tf_op jit(solution)/shard_map/finish/pallas_call | solution.py:415
